TPU v7x, 512 devices: a whole 4x8x8 slice. The times are simulated.
512 devices in a mesh: gz: 128 (over y_lo, z, x), gy: 4 (over y_hi, core).
Axes of the slice: x: 4, y: 8 (y_hi: 2, y_lo: 4; y = y_hi * 4 + y_lo), z: 8, core: 2. Of those that a mesh axis runs over, the one named last changes fastest.
Arguments:
- volume: bfloat16 [512, 16, 32, 128], P('gz', 'gy'), may hold values from -6 to 6
- kernel_a: bfloat16 [3, 3, 3, 128, 128], replicated, may hold values from -0.109375 to 0.109375
- bias_a: float32 [128], replicated, may hold values from -3 to 3
- kernel_b: bfloat16 [3, 3, 3, 128, 256], P(None, None, None, None, 'gy'), may hold values from -0.109375 to 0.109375
- bias_b: float32 [256], P('gy'), may hold values from -3 to 3
- kernel_c: bfloat16 [3, 3, 3, 256, 512], P(None, None, None, None, 'gy'), may hold values from -0.078125 to 0.078125
- bias_c: float32 [512], P('gy'), may hold values from -3 to 3
Outputs:
- skip_a: bfloat16 [512, 16, 32, 128], P('gz', 'gy')
- skip_b: bfloat16 [256, 8, 16, 256], P('gz', None, None, 'gy')
- bottom: bfloat16 [128, 4, 8, 512], P('gz', None, None, 'gy')
All inputs are finite; a program needn't handle non-finite values.
Results may differ from a plain program's by a relative error of at most 0.0054.
Values may be sent and summed in bfloat16 or wider, within the bound.
No kernel may reach another device: no remote copies, remote signals or barrier semaphores. Data moves between devices by JAX's collectives and lax.ppermute only.
A program may use at most 64 MiB of HBM per device.

v0:
```python
import jax
import jax.numpy as jnp
from jax import lax
from jax.sharding import PartitionSpec as P


def even_groups(peers):
    return [[i, i + 1] for i in range(0, peers, 2)]


def odd_pairs(peers):
    pairs = [(i, i + 1) for i in range(1, peers - 1, 2)]
    return pairs + [(j, i) for i, j in pairs]


def swapped(field, axis, dim, width):
    peers, length = lax.axis_size(axis), field.shape[dim]
    odd = lax.axis_index(axis) % 2
    room = length - width
    outward = lax.dynamic_slice_in_dim(field, odd * room, width, dim)
    inward = lax.dynamic_slice_in_dim(field, (1 - odd) * room, width, dim)
    across = lax.ppermute(outward, axis, odd_pairs(peers))
    pair = lax.all_gather(inward, axis, axis_index_groups=even_groups(peers))
    partner = lax.dynamic_index_in_dim(pair, 1 - odd, 0, keepdims=False)
    before = jnp.where(odd == 1, partner, across)
    after = jnp.where(odd == 1, across, partner)
    return jnp.concatenate([before, field, after], axis=dim)


def conv_relu(padded, kernel, bias):
    out = lax.conv_general_dilated(
        padded[None],
        kernel,
        (1, 1, 1),
        ((0, 0), (0, 0), (1, 1)),
        dimension_numbers=("NDHWC", "DHWIO", "NDHWC"),
        preferred_element_type=jnp.float32,
    )[0]
    return jnp.maximum(out + bias, 0.0).astype(jnp.bfloat16)


def shrink(field):
    depth, height, width, chans = field.shape
    blocks = field.reshape(depth // 2, 2, height // 2, 2, width // 2, 2, chans)
    return jnp.max(blocks, axis=(1, 3, 5))


def pad_height(field):
    return jnp.pad(field, ((0, 0), (1, 1), (0, 0), (0, 0)))


def levels(volume, kernel_a, bias_a, kernel_b, bias_b, kernel_c, bias_c):
    gz, last = lax.axis_index("gz"), lax.axis_size("gz") - 1
    wide = swapped(volume, "gz", 0, 3)
    padded = swapped(wide, "gy", 1, 1)
    full_a = conv_relu(padded, kernel_a, bias_a)
    skip_a = full_a[2:6]
    pooled_a = shrink(full_a)
    layer = lax.broadcasted_iota(jnp.int32, (4, 1, 1, 1), 0)
    outside = ((gz == 0) & (layer == 0)) | ((gz == last) & (layer == 3))
    pooled_a = jnp.where(outside, jnp.bfloat16(0), pooled_a)
    ready_b = lax.all_gather(pooled_a, "gy", axis=1, tiled=True)
    skip_b = conv_relu(pad_height(ready_b), kernel_b, bias_b)
    pooled_b = swapped(shrink(skip_b), "gz", 0, 1)
    shards = lax.all_gather(pooled_b, "gy")
    ready_c = jnp.moveaxis(shards, 0, 3).reshape(3, 4, 8, -1)
    bottom = conv_relu(pad_height(ready_c), kernel_c, bias_c)
    return (skip_a, skip_b, bottom)


def solution(mesh):
    return jax.shard_map(
        levels,
        mesh=mesh,
        in_specs=(
            P("gz", "gy", None, None),
            P(),
            P(),
            P(None, None, None, None, "gy"),
            P("gy"),
            P(None, None, None, None, "gy"),
            P("gy"),
        ),
        out_specs=(P("gz", "gy", None, None), P("gz", None, None, "gy"), P("gz", None, None, "gy")),
        check_vma=False,
    )
```

profile of v0, /device:TPU:57, one launch (start us, length us, event | category | flops | bytes accessed | tf_op | source)
XLA Modules:
  0.0 74.0 jit_solution(15464261595027324774)
XLA Ops:
  0.6 0.0 copy-start
  0.6 0.0 copy-start.1
  0.7 1.1 %constant_dynamic-slice_fusion.4 = (bf16[3,4,32,128]{3,2,1,0:T(8,128)(2,1)S(1)}, bf16[3,4,32,128]{3,2,1,0:T(8,128)(2,1)S(1)}) fusion(bf16[4,4,32,128]{3,2,1,0:T(8,128)(2,1)} %param.7, s32[]{:T(128)S(6)} %select_n.79, s32[]{:T(128)S(6)} %select_n.81), kind=kLoop, calls=%fused_computation.50 | loop fusion | bytes 393224 | tf_op jit(solution)/shard_map/dynamic_slice | solution.py:21
  1.8 13.6 %collective-permute-start = (bf16[3,4,32,128]{3,2,1,0:T(8,128)(2,1)S(1)}, bf16[3,4,32,128]{3,2,1,0:T(8,128)(2,1)S(1)}, u32[]{:S(2)}, u32[]{:S(2)}) collective-permute-start(bf16[3,4,32,128]{3,2,1,0:T(8,128)(2,1)S(1)} %get-tuple-element.24), channel_id=1, source_target_pairs={{4,8},{12,16},{20,24},{28,32},{36,40},{44,48},{52,56},{60,64},{68,... | collective-permute-start | bytes 294920 | tf_op jit(solution)/shard_map/ppermute | solution.py:22
  15.5 4.1 %all-gather = bf16[6,4,32,128]{3,2,1,0:T(8,128)(2,1)S(1)} all-gather(bf16[3,4,32,128]{3,2,1,0:T(8,128)(2,1)S(1)} %get-tuple-element.23), channel_id=2, replica_groups={{0,4},{8,12},{16,20},{24,28},{32,36},{40,44},{48,52},{56,60},{64,68},{7..., dimensions={0}, use_global_device_ids=true | all-gather | bytes 294912 | tf_op jit(solution)/shard_map/all_gather | solution.py:23
  19.6 0.0 collective-permute-done
  19.7 0.9 %pad_maximum_fusion = bf16[10,4,32,128]{3,2,1,0:T(8,128)(2,1)S(1)} fusion(bf16[3,4,32,128]{3,2,1,0:T(8,128)(2,1)S(1)} %get-tuple-element.20, bf16[4,4,32,128]{3,2,1,0:T(8,128)(2,1)} %param.7, bf16[3,4,32,128]{3,2,1,0:T(8,128)(2,1)S(1)} %get-tuple-element.19), kind=kLoop, calls=%fused_computation.19 | loop fusion | flops 327680 | bytes 655360 | tf_op jit(solution)/shard_map/concatenate | solution.py:27
  20.6 0.7 collective-permute-start.1
  21.3 4.9 %all-gather.1 = bf16[20,1,32,128]{3,2,1,0:T(8,128)(2,1)S(1)} all-gather(bf16[10,1,32,128]{3,2,1,0:T(8,128)(2,1)S(1)} %get-tuple-element.17), channel_id=3, replica_groups={{0,1},{2,3},{4,5},{6,7},{8,9},{10,11},{12,13},{14,15},{16,17},{18,19},{..., dimensions={0}, use_global_device_ids=true | all-gather | bytes 245760 | tf_op jit(solution)/shard_map/all_gather | solution.py:23
  26.3 0.0 collective-permute-done.1
  26.3 0.0 copy-done.1
  26.3 0.1 maximum_bitcast_fusion
  26.4 0.2 copy.73
  26.6 0.0 copy-start.5
  26.6 0.0 copy-start.7
  26.6 0.2 pad.10.clone
  26.8 0.1 copy.57
  26.9 0.1 slice.9
  27.0 0.8 %copy-done.5 = bf16[3,3,3,128,128]{4,3,2,1,0:T(8,128)(2,1)S(1)} copy-done((bf16[3,3,3,128,128]{4,3,2,1,0:T(8,128)(2,1)S(1)}, bf16[3,3,3,128,128]{4,3,2,1,0:T(8,128)(2,1)}, u32[]{:S(2)}) %copy-start.5) | copy-done | bytes 884760
  27.8 0.0 copy-done.7
  27.8 2.5 %convolution_select_fusion = f32[8,4,8,5,128]{4,2,3,1,0:T(8,128)S(1)} fusion(bf16[3,3,3,128,128]{4,3,2,1,0:T(8,128)(2,1)S(1)} %copy-done.5, bf16[10,6,1,7,2,128]{5,3,4,1,0,2:T(8,128)(2,1)S(1)} %slice.9, bf16[10,6,1,8,5,128]{5,3,4,1,0,2:T(8,128)(2,1)S(1)} %copy.57, pred[8,5]{0,1:T(8,128)(4,1)S(1)} %copy-done.7), kind=kOutput, calls=%fused_computation.2 | convolution fusion | flops 1135206400 | bytes 2369576 | tf_op jit(solution)/shard_map/conv_general_dilated | solution.py:31
  30.3 0.0 copy-start.2
  30.3 0.4 copy.58
  30.7 0.1 fusion.30
  30.8 0.0 copy-start.3
  30.8 0.0 copy-start.6
  30.8 0.0 copy-start.8
  30.8 0.1 copy-done.2
  31.0 0.4 fusion.17
  31.3 0.1 fusion.16
  31.4 0.1 broadcast_select_fusion
  31.6 16.1 %all_gather.31 = bf16[4,8,16,128]{3,2,0,1:T(8,128)(2,1)S(1)} all-gather(bf16[4,2,16,128]{3,2,0,1:T(8,128)(2,1)S(1)} %copy.59), channel_id=1, replica_groups=mesh['gz'=128,'gy'=4] {'gy'}, dimensions={1}, use_global_device_ids=true | all-gather | bytes 163840 | tf_op jit(solution)/shard_map/all_gather | solution.py:62
  47.7 0.1 copy.74
  47.8 0.1 pad.12.clone
  47.9 0.0 copy-done.3
  48.0 0.0 copy-done.6
  48.0 0.0 copy-done.8
  48.0 0.8 %maximum_convert_fusion.1 = (bf16[2,8,8,3,64]{4,2,3,1,0:T(8,128)(2,1)S(1)}, f32[2,8,8,3,64]{4,2,3,1,0:T(8,128)S(1)}) fusion(f32[64]{0:T(128)S(1)} %copy-done.3, bf16[3,3,3,128,64]{3,4,2,1,0:T(8,128)(2,1)S(1)} %copy-done.6, bf16[4,10,1,7,2,128]{5,3,4,1,0,2:T(8,128)(2,1)S(1)} %slice.12, bf16[4,10,1,8,3,128]{5,3,4,1,0,2:T(8,128)(2,1)S(1)} %copy.62, ...), kind=kOutput, calls=%fused_computation.25 | convolution fusion | flops 171196416 | bytes 979224 | tf_op jit(solution)/shard_map/conv_general_dilated | solution.py:31
  48.9 0.1 reduce_max.30
  49.0 3.2 %all-gather.2 = bf16[8,8,64]{2,1,0:T(8,128)(2,1)S(1)} all-gather(bf16[4,8,64]{2,1,0:T(8,128)(2,1)S(1)} %copy.65), channel_id=4, replica_groups={{0,4},{8,12},{16,20},{24,28},{32,36},{40,44},{48,52},{56,60},{64,68},{7..., dimensions={0}, use_global_device_ids=true | all-gather | bytes 12288 | tf_op jit(solution)/shard_map/all_gather | solution.py:23
  52.2 4.3 %collective-permute-start.2 = (bf16[1,4,8,64]{3,1,2,0:T(4,128)(2,1)S(1)}, bf16[1,4,8,64]{3,1,2,0:T(4,128)(2,1)S(1)}, u32[]{:S(2)}, u32[]{:S(2)}) collective-permute-start(bf16[1,4,8,64]{3,1,2,0:T(4,128)(2,1)S(1)} %bitcast.66), channel_id=1, source_target_pairs={{4,8},{12,16},{20,24},{28,32},{36,40},{44,48},{52,56},{60,64},{68,... | collective-permute-start | bytes 12296 | tf_op jit(solution)/shard_map/ppermute | solution.py:22
  56.6 0.7 copy.70
  57.2 0.6 copy.71
  57.9 2.9 %collective-permute-done.2 = bf16[1,4,8,64]{3,1,2,0:T(4,128)(2,1)S(1)} collective-permute-done((bf16[1,4,8,64]{3,1,2,0:T(4,128)(2,1)S(1)}, bf16[1,4,8,64]{3,1,2,0:T(4,128)(2,1)S(1)}, u32[]{:S(2)}, u32[]{:S(2)}) %collective-permute-start.2) | collective-permute-done | bytes 4128 | tf_op jit(solution)/shard_map/ppermute | solution.py:22
  60.8 0.0 copy-start.4
  60.9 11.7 %all-gather.3 = bf16[12,4,8,64]{3,2,1,0:T(8,128)(2,1)S(1)} all-gather(bf16[3,4,8,64]{3,2,1,0:T(8,128)(2,1)S(1)} %copy.67), channel_id=5, replica_groups=mesh['gz'=128,'gy'=4] {'gy'}, dimensions={0}, use_global_device_ids=true | all-gather | bytes 61440 | tf_op jit(solution)/shard_map/all_gather | solution.py:65
  72.6 0.1 copy.68
  72.7 0.1 reshape.58
  72.8 0.0 copy-done
  72.8 0.6 fusion.19
  73.4 0.0 copy-done.4
  73.4 0.6 maximum_convert_fusion.2
  (18 shorter events, 0.3 us)
Async XLA Ops:
  0.6 72.2 %copy-start = (bf16[3,3,3,256,128]{4,3,2,1,0:T(8,128)(2,1)S(1)}, bf16[3,3,3,256,128]{4,3,2,1,0:T(8,128)(2,1)}, u32[]{:S(2)}) copy-start(bf16[3,3,3,256,128]{4,3,2,1,0:T(8,128)(2,1)} %param.12) | copy-start | bytes 5308420
  0.6 25.6 %copy-start.1 = (bf16[4,4,32,128]{3,2,1,0:T(8,128)(2,1)S(1)}, bf16[4,4,32,128]{3,2,1,0:T(8,128)(2,1)}, u32[]{:S(2)}) copy-start(bf16[4,4,32,128]{3,2,1,0:T(8,128)(2,1)} %param.7) | copy-start | bytes 393220
  1.8 17.8 %collective-permute-start = (bf16[3,4,32,128]{3,2,1,0:T(8,128)(2,1)S(1)}, bf16[3,4,32,128]{3,2,1,0:T(8,128)(2,1)S(1)}, u32[]{:S(2)}, u32[]{:S(2)}) collective-permute-start(bf16[3,4,32,128]{3,2,1,0:T(8,128)(2,1)S(1)} %get-tuple-element.24), channel_id=1, source_target_pairs={{4,8},{12,16},{20,24},{28,32},{36,40},{44,48},{52,56},{60,64},{68,... | collective-permute-start | bytes 294920 | tf_op jit(solution)/shard_map/ppermute | solution.py:22
  20.6 5.6 %collective-permute-start.1 = (bf16[10,1,32,128]{3,2,1,0:T(8,128)(2,1)S(1)}, bf16[10,1,32,128]{3,2,1,0:T(8,128)(2,1)S(1)}, u32[]{:S(2)}, u32[]{:S(2)}) collective-permute-start(bf16[10,1,32,128]{3,2,1,0:T(8,128)(2,1)S(1)} %get-tuple-element.18), channel_id=1, source_target_pairs={{1,2},{2,1},{5,6},{6,5},{9,10},{10,9},{13,14},{14,13},{17,18},{18,... | collective-permute-start | bytes 245768 | tf_op jit(solution)/shard_map/ppermute | solution.py:22
  26.6 1.2 %copy-start.5 = (bf16[3,3,3,128,128]{4,3,2,1,0:T(8,128)(2,1)S(1)}, bf16[3,3,3,128,128]{4,3,2,1,0:T(8,128)(2,1)}, u32[]{:S(2)}) copy-start(bf16[3,3,3,128,128]{4,3,2,1,0:T(8,128)(2,1)} %param.8) | copy-start | bytes 2654212
  26.6 1.2 %copy-start.7 = (pred[8,5]{0,1:T(8,128)(4,1)S(1)}, pred[8,5]{0,1:T(8,128)(4,1)}, u32[]{:S(2)}) copy-start(pred[8,5]{0,1:T(8,128)(4,1)} %constant.76) | copy-start | bytes 124
  30.3 0.7 copy-start.2
  30.8 17.2 %copy-start.3 = (f32[64]{0:T(128)S(1)}, f32[64]{0:T(128)}, u32[]{:S(2)}) copy-start(f32[64]{0:T(128)} %param.11) | copy-start | bytes 772
  30.8 17.2 %copy-start.6 = (bf16[3,3,3,128,64]{3,4,2,1,0:T(8,128)(2,1)S(1)}, bf16[3,3,3,128,64]{3,4,2,1,0:T(8,128)(2,1)}, u32[]{:S(2)}) copy-start(bf16[3,3,3,128,64]{3,4,2,1,0:T(8,128)(2,1)} %param.10) | copy-start | bytes 1327108
  30.8 17.2 %copy-start.8 = (pred[8,3]{0,1:T(4,128)(4,1)S(1)}, pred[8,3]{0,1:T(4,128)(4,1)}, u32[]{:S(2)}) copy-start(pred[8,3]{0,1:T(4,128)(4,1)} %constant.77) | copy-start | bytes 76
  52.2 8.6 %collective-permute-start.2 = (bf16[1,4,8,64]{3,1,2,0:T(4,128)(2,1)S(1)}, bf16[1,4,8,64]{3,1,2,0:T(4,128)(2,1)S(1)}, u32[]{:S(2)}, u32[]{:S(2)}) collective-permute-start(bf16[1,4,8,64]{3,1,2,0:T(4,128)(2,1)S(1)} %bitcast.66), channel_id=1, source_target_pairs={{4,8},{12,16},{20,24},{28,32},{36,40},{44,48},{52,56},{60,64},{68,... | collective-permute-start | bytes 12296 | tf_op jit(solution)/shard_map/ppermute | solution.py:22
  60.8 12.6 %copy-start.4 = (f32[128]{0:T(128)S(1)}, f32[128]{0:T(128)}, u32[]{:S(2)}) copy-start(f32[128]{0:T(128)} %param.13) | copy-start | bytes 1540
where the time goes:
time: 74.3 us; the launch traced here: 74 us
  blocking collectives  40.1 us (54%)
  starting transfers between devices  18.6 us (25%)
  local copies, waits for them, and re-layouts  4.95 us (7%)
  matrix products  3.93 us (5%)
  waiting for transfers between devices  2.91 us (4%)
  other arithmetic  2.39 us (3%)
  between operations  1.1 us (1%)
    ppermute x3, starting transfers between devices, swapped(): across = lax.ppermute(outward, axis, odd_pairs(peers))  18.6 us
    all_gather x1, blocking collectives, levels(): ready_b = lax.all_gather(pooled_a, 'gy', axis=1, tiled=True)  16.1 us
    all_gather x3, blocking collectives, swapped(): pair = lax.all_gather(inward, axis, axis_index_groups=even_groups(peers))  12.3 us
    all_gather x1, blocking collectives, levels(): shards = lax.all_gather(pooled_b, 'gy')  11.7 us
    conv_general_dilated x3, matrix products, conv_relu(): lax.conv_general_dilated(padded[None], kernel, (1, 1, 1), ((0, 0), (0, 0)...  3.93 us
    ppermute x3, waiting for transfers between devices, swapped(): across = lax.ppermute(outward, axis, odd_pairs(peers))  2.91 us
    unnamed x22, local copies, waits for them, and re-layouts  2.61 us
  transfers between devices with their start and end apart: 3, of which 1 were waited for; matrix products, arithmetic and copies ran while one was open for 2% of the time, Pallas kernels for 0%

commit v1 on v0

v1 whole, which is shorter than its diff:
```python
import jax
import jax.numpy as jnp
from jax import lax
from jax.experimental import pallas as pl
from jax.experimental.pallas import tpu as pltpu
from jax.sharding import PartitionSpec as P

BF16, F32 = jnp.bfloat16, jnp.float32


def even_groups(peers):
    return [[i, i + 1] for i in range(0, peers, 2)]


def odd_pairs(peers):
    pairs = [(i, i + 1) for i in range(1, peers - 1, 2)]
    return pairs + [(j, i) for i, j in pairs]


def swap(outward, inward, axis):
    peers = lax.axis_size(axis)
    across = lax.ppermute(outward, axis, odd_pairs(peers))
    pair = lax.all_gather(inward, axis, axis_index_groups=even_groups(peers))
    return pair, across


def ends(field, axis, width):
    odd = lax.axis_index(axis) % 2
    room = field.shape[0] - width
    outward = lax.dynamic_slice_in_dim(field, odd * room, width, 0)
    inward = lax.dynamic_slice_in_dim(field, (1 - odd) * room, width, 0)
    return outward, inward


def local(body, inputs, outs, scratch=(), flops=0):
    spec = pl.BlockSpec(memory_space=pltpu.VMEM)
    return pl.pallas_call(
        body,
        out_shape=[jax.ShapeDtypeStruct(shape, BF16) for shape in outs],
        in_specs=[spec] * len(inputs),
        out_specs=[spec] * len(outs),
        scratch_shapes=[pltpu.VMEM(shape, dtype) for shape, dtype in scratch],
        cost_estimate=pl.CostEstimate(flops=flops, bytes_accessed=1 << 20, transcendentals=0),
        compiler_params=pltpu.CompilerParams(vmem_limit_bytes=32 << 20),
    )(*inputs)


def three_taps(wide, width, chans):
    cells = wide.shape[0]
    column = lax.broadcasted_iota(jnp.int32, (cells, chans), 0) % width
    left = jnp.where(column == 0, 0.0, pltpu.roll(wide[:, :chans], 1, 0))
    right = jnp.where(column == width - 1, 0.0, pltpu.roll(wide[:, 2 * chans :], cells - 1, 0))
    return left + wide[:, chans : 2 * chans] + right


TAPS = [(i, j) for i in range(3) for j in range(3)]


def join(volume, pair, across, wide, outward, inward):
    odd, core = lax.axis_index("gz") % 2, lax.axis_index("gy") % 2
    wide[3:7] = volume[...]
    wide[pl.ds(7 * (1 - odd), 3)] = pair[1 - odd]
    wide[pl.ds(7 * odd, 3)] = across[...]
    outward[...] = wide[:, 3 * core]
    inward[...] = wide[:, 3 * (1 - core)]


def level_a(wide, pair, across, kernel, bias, skip, pooled, x, most):
    core = lax.axis_index("gy") % 2
    x[:, 1:5] = wide[...]
    x[:, 5 * (1 - core)] = pair[1 - core]
    x[:, 5 * core] = across[...]
    weights = jnp.concatenate(
        [jnp.concatenate([kernel[i, j, tap] for tap in range(3)], axis=1) for i, j in TAPS], axis=0
    )
    for p in (1, 2, 0, 3):
        z = 2 * p
        cells = jnp.concatenate([x[z + i : z + i + 2, j : j + 4].reshape(256, 128) for i, j in TAPS], axis=1)
        sums = jnp.dot(cells, weights, preferred_element_type=F32)
        out = jnp.maximum(three_taps(sums, 32, 128) + bias[...], 0.0)
        if p in (1, 2):
            skip[z - 2 : z] = out.astype(BF16).reshape(2, 4, 32, 128)
        most[...] = jnp.max(out.reshape(2, 2, 2, 32, 128), axis=(0, 2)).reshape(64, 128)
        small = jnp.maximum(most[pl.ds(0, 32, stride=2)], most[pl.ds(1, 32, stride=2)])
        pooled[p] = small.astype(BF16).reshape(2, 16, 128)


def level_b(shards, kernel, bias, skip, pooled, x, most):
    gz = lax.axis_index("gz")
    x[:, 0] = jnp.zeros((4, 16, 128), BF16)
    x[:, 9] = jnp.zeros((4, 16, 128), BF16)
    for g in range(4):
        x[:, 2 * g + 1 : 2 * g + 3] = shards[g]

    @pl.when(gz == 0)
    def _():
        x[0] = jnp.zeros((10, 16, 128), BF16)

    @pl.when(gz == lax.axis_size("gz") - 1)
    def _():
        x[3] = jnp.zeros((10, 16, 128), BF16)

    weights = jnp.concatenate(
        [jnp.concatenate([kernel[i, j, tap] for tap in range(3)], axis=0) for i, j in TAPS], axis=1
    )
    cells = jnp.concatenate([x[i : i + 2, j : j + 8].reshape(256, 128) for i, j in TAPS], axis=1)
    sums = lax.dot_general(cells, weights, (((1,), (1,)), ((), ())), preferred_element_type=F32)
    out = jnp.maximum(three_taps(sums, 16, 64) + bias[...], 0.0)
    skip[...] = out.astype(BF16).reshape(2, 8, 16, 64)
    most[...] = jnp.max(out.reshape(2, 4, 2, 16, 64), axis=(0, 2)).reshape(64, 64)
    small = jnp.maximum(most[pl.ds(0, 32, stride=2)], most[pl.ds(1, 32, stride=2)])
    pooled[...] = small.astype(BF16).reshape(1, 4, 8, 64)


def level_c(shards, kernel, bias, bottom, x):
    x[:, 0] = jnp.zeros((3, 8, 256), BF16)
    x[:, 5] = jnp.zeros((3, 8, 256), BF16)
    x[:, 1:5] = jnp.concatenate([shards[g] for g in range(4)], axis=-1)
    weights = jnp.concatenate(
        [jnp.concatenate([kernel[i, j, tap] for tap in range(3)], axis=1) for i, j in TAPS], axis=0
    )
    cells = jnp.concatenate([x[i, j : j + 4].reshape(32, 256) for i, j in TAPS], axis=1)
    sums = jnp.dot(cells, weights, preferred_element_type=F32)
    out = jnp.maximum(three_taps(sums, 8, 128) + bias[...], 0.0)
    bottom[...] = out.astype(BF16).reshape(1, 4, 8, 128)


def levels(volume, kernel_a, bias_a, kernel_b, bias_b, kernel_c, bias_c):
    pair, across = swap(*ends(volume, "gz", 3), "gz")
    wide, outward, inward = local(join, (volume, pair, across), [(10, 4, 32, 128), (10, 32, 128), (10, 32, 128)])
    pair, across = swap(outward, inward, "gy")
    skip_a, pooled_a = local(
        level_a,
        (wide, pair, across, kernel_a, bias_a[None]),
        [(4, 4, 32, 128), (4, 2, 16, 128)],
        [((10, 6, 32, 128), BF16), ((64, 128), F32)],
        1 << 30,
    )
    skip_b, pooled_b = local(
        level_b,
        (lax.all_gather(pooled_a, "gy"), jnp.swapaxes(kernel_b, 3, 4), bias_b[None]),
        [(2, 8, 16, 64), (1, 4, 8, 64)],
        [((4, 10, 16, 128), BF16), ((64, 64), F32)],
        1 << 28,
    )
    pair, across = swap(pooled_b, pooled_b, "gz")
    odd = lax.axis_index("gz") % 2
    partner = lax.dynamic_index_in_dim(pair, 1 - odd, 0, keepdims=False)
    deep = jnp.concatenate([jnp.where(odd == 1, partner, across), pooled_b, jnp.where(odd == 1, across, partner)])
    (bottom,) = local(
        level_c,
        (lax.all_gather(deep, "gy"), kernel_c, bias_c[None]),
        [(1, 4, 8, 128)],
        [((3, 6, 8, 256), BF16)],
        1 << 27,
    )
    return (skip_a, skip_b, bottom)


def solution(mesh):
    return jax.shard_map(
        levels,
        mesh=mesh,
        in_specs=(
            P("gz", "gy", None, None),
            P(),
            P(),
            P(None, None, None, None, "gy"),
            P("gy"),
            P(None, None, None, None, "gy"),
            P("gy"),
        ),
        out_specs=(P("gz", "gy", None, None), P("gz", None, None, "gy"), P("gz", None, None, "gy")),
        check_vma=False,
    )
```

time: 74.3 us -> 67.5 us (0.908)
  Pallas kernels: 0 us -> 4.07 us
  matrix products: 3.93 us -> 0 us
  other arithmetic: 2.39 us -> 0.02 us
  waiting for transfers between devices: 2.91 us -> 0.8 us
  local copies, waits for them, and re-layouts: 4.95 us -> 3.73 us
  blocking collectives: 40.1 us -> 39.2 us
    pallas_call x0 -> x4, Pallas kernels: none -> 4.07 us  [local(): pl.pallas_call(body, out_shape=[jax.ShapeDtypeStruct(shape, BF16) for sha...]
    conv_general_dilated x3 -> x0, matrix products: 3.93 us -> none  [conv_relu(): lax.conv_general_dilated(padded[None], kernel, (1, 1, 1), ((0, 0), (0, 0)...]
    ppermute x3, waiting for transfers between devices: 2.91 us -> 0.8 us  [swap(): across = lax.ppermute(outward, axis, odd_pairs(peers))]
    concatenate x2 -> x1, other arithmetic: 0.97 us -> 0.01 us  [levels(): jnp.concatenate([jnp.where(odd == 1, partner, across), pooled_b, jnp.wher...]
    all_gather x5, blocking collectives: 40.1 us -> 39.2 us  [the longest x1 16.1 us: levels(): lax.all_gather(pooled_a, 'gy')]
    unnamed x22 -> x14, local copies, waits for them, and re-layouts: 2.61 us -> 2.74 us
  transfers between devices with their start and end apart: 3 -> 3, of which waited for: 1 -> 1; matrix products, arithmetic and copies ran while one was open for 2% -> 0% of each run, Pallas kernels for 0% -> 0%
where the time goes in v1:
time: 67.5 us; the launch traced here: 67.2 us
  blocking collectives  39.2 us (58%)
  starting transfers between devices  18.6 us (28%)
  Pallas kernels  4.07 us (6%)
  local copies, waits for them, and re-layouts  3.73 us (6%)
  waiting for transfers between devices  0.8 us (1%)
  between operations  0.71 us (1%)
    ppermute x3, starting transfers between devices, swap(): across = lax.ppermute(outward, axis, odd_pairs(peers))  18.6 us
    all_gather x1, blocking collectives, levels(): lax.all_gather(pooled_a, 'gy')  16.1 us
    all_gather x3, blocking collectives, swap(): pair = lax.all_gather(inward, axis, axis_index_groups=even_groups(peers))  12.5 us
    all_gather x1, blocking collectives, levels(): lax.all_gather(deep, 'gy')  10.6 us
    pallas_call x4, Pallas kernels, local(): pl.pallas_call(body, out_shape=[jax.ShapeDtypeStruct(shape, BF16) for sha...  4.07 us
    unnamed x14, local copies, waits for them, and re-layouts  2.74 us
  transfers between devices with their start and end apart: 3, of which 1 were waited for; matrix products, arithmetic and copies ran while one was open for 0% of the time, Pallas kernels for 0%

profile of v1, /device:TPU:57, one launch (start us, length us, event | category | flops | bytes accessed | tf_op | source)
XLA Modules:
  0.0 67.2 jit_solution(17287483725794103586)
XLA Ops:
  0.7 1.0 %constant_dynamic-slice_fusion = (bf16[3,4,32,128]{3,2,1,0:T(8,128)(2,1)S(1)}, bf16[3,4,32,128]{3,2,1,0:T(8,128)(2,1)S(1)}) fusion(bf16[4,4,32,128]{3,2,1,0:T(8,128)(2,1)} %volume.1, s32[]{:T(128)S(6)} %select_n.33, s32[]{:T(128)S(6)} %select_n.32), kind=kLoop, calls=%fused_computation.3 | loop fusion | bytes 393224 | tf_op jit(solution)/shard_map/dynamic_slice | solution.py:30
  1.6 13.6 %collective-permute-start = (bf16[3,4,32,128]{3,2,1,0:T(8,128)(2,1)S(1)}, bf16[3,4,32,128]{3,2,1,0:T(8,128)(2,1)S(1)}, u32[]{:S(2)}, u32[]{:S(2)}) collective-permute-start(bf16[3,4,32,128]{3,2,1,0:T(8,128)(2,1)S(1)} %get-tuple-element.17), channel_id=1, source_target_pairs={{4,8},{12,16},{20,24},{28,32},{36,40},{44,48},{52,56},{60,64},{68,... | collective-permute-start | bytes 294920 | tf_op jit(solution)/shard_map/ppermute | solution.py:22
  15.3 4.1 %all-gather = bf16[6,4,32,128]{3,2,1,0:T(8,128)(2,1)S(1)} all-gather(bf16[3,4,32,128]{3,2,1,0:T(8,128)(2,1)S(1)} %get-tuple-element.18), channel_id=2, replica_groups={{0,4},{8,12},{16,20},{24,28},{32,36},{40,44},{48,52},{56,60},{64,68},{7..., dimensions={0}, use_global_device_ids=true | all-gather | bytes 294912 | tf_op jit(solution)/shard_map/all_gather | solution.py:23
  19.4 0.0 collective-permute-done.across
  19.4 0.0 copy-start.1
  19.4 0.9 %copy-done.1 = bf16[4,4,32,128]{3,2,1,0:T(8,128)(2,1)S(1)} copy-done((bf16[4,4,32,128]{3,2,1,0:T(8,128)(2,1)S(1)}, bf16[4,4,32,128]{3,2,1,0:T(8,128)(2,1)}, u32[]{:S(2)}) %copy-start.1) | copy-done | bytes 131096
  20.4 0.7 collective-permute-start.1
  21.1 4.9 %all-gather.1 = bf16[20,32,128]{2,1,0:T(8,128)(2,1)S(1)} all-gather(bf16[10,32,128]{2,1,0:T(8,128)(2,1)S(1)} %get-tuple-element.11), channel_id=3, replica_groups={{0,1},{2,3},{4,5},{6,7},{8,9},{10,11},{12,13},{14,15},{16,17},{18,19},{..., dimensions={0}, use_global_device_ids=true | all-gather | bytes 245760 | tf_op jit(solution)/shard_map/all_gather | solution.py:23
  26.0 0.0 collective-permute-done.1.across
  26.0 0.0 copy-start.3
  26.0 1.2 %copy-done.3 = bf16[3,3,3,128,128]{4,3,2,1,0:T(8,128)(2,1)S(1)} copy-done((bf16[3,3,3,128,128]{4,3,2,1,0:T(8,128)(2,1)S(1)}, bf16[3,3,3,128,128]{4,3,2,1,0:T(8,128)(2,1)}, u32[]{:S(2)}) %copy-start.3) | copy-done | bytes 884760
  27.2 0.0 copy-start.5
  27.2 0.7 copy-done.5
  27.8 0.0 copy-start.4
  27.8 0.0 copy-start.6
  27.8 0.0 copy-start
  27.8 0.0 copy-start.2
  27.8 1.9 %shard_map.95 = (bf16[4,4,32,128]{3,2,1,0:T(8,128)(2,1)}, bf16[4,2,16,128]{3,2,1,0:T(8,128)(2,1)S(1)}) custom-call(bf16[10,4,32,128]{3,2,1,0:T(8,128)(2,1)S(1)} %get-tuple-element.10.wide, bf16[2,10,32,128]{3,2,1,0:T(8,128)(2,1)S(1)} %bitcast.10, bf16[10,32,128]{2,1,0:T(8,128)(2,1)S(1)} %collective-permute-done.1.across, ...), custom_call_target="tpu_custom_call" | custom-call | flops 1073741824 | bytes 1048576 | tf_op jit(solution)/shard_map/pallas_call | solution.py:37
  29.8 16.1 %all-gather.2 = bf16[16,2,16,128]{3,2,1,0:T(8,128)(2,1)S(1)} all-gather(bf16[4,2,16,128]{3,2,1,0:T(8,128)(2,1)S(1)} %get-tuple-element.14), channel_id=4, replica_groups=mesh['gz'=128,'gy'=4] {'gy'}, dimensions={0}, use_global_device_ids=true | all-gather | bytes 163840 | tf_op jit(solution)/shard_map/all_gather | solution.py:141
  45.9 0.0 copy-done.4
  45.9 0.0 copy-done.6
  45.9 1.1 %shard_map.96 = (bf16[2,8,16,64]{3,2,1,0:T(8,128)(2,1)}, bf16[1,4,8,64]{3,2,1,0:T(8,128)(2,1)S(1)}) custom-call(bf16[4,4,2,16,128]{4,3,2,1,0:T(8,128)(2,1)S(1)} %bitcast.11, bf16[3,3,3,64,128]{4,3,2,1,0:T(8,128)(2,1)S(1)} %bitcast.13, f32[1,64]{1,0:T(1,128)S(1)} %bitcast.15), custom_call_target="tpu_custom_call" | custom-call | flops 268435456 | bytes 1048576 | tf_op jit(solution)/shard_map/pallas_call | solution.py:37
  47.0 4.3 %collective-permute-start.2 = (bf16[1,4,8,64]{3,2,1,0:T(8,128)(2,1)S(1)}, bf16[1,4,8,64]{3,2,1,0:T(8,128)(2,1)S(1)}, u32[]{:S(2)}, u32[]{:S(2)}) collective-permute-start(bf16[1,4,8,64]{3,2,1,0:T(8,128)(2,1)S(1)} %get-tuple-element.16), channel_id=1, source_target_pairs={{4,8},{12,16},{20,24},{28,32},{36,40},{44,48},{52,56},{60,64},{68,... | collective-permute-start | bytes 12296 | tf_op jit(solution)/shard_map/ppermute | solution.py:22
  51.3 3.5 %all-gather.3 = bf16[2,4,8,64]{3,2,1,0:T(8,128)(2,1)S(1)} all-gather(bf16[1,4,8,64]{3,2,1,0:T(8,128)(2,1)S(1)} %get-tuple-element.16), channel_id=5, replica_groups={{0,4},{8,12},{16,20},{24,28},{32,36},{40,44},{48,52},{56,60},{64,68},{7..., dimensions={0}, use_global_device_ids=true | all-gather | bytes 12288 | tf_op jit(solution)/shard_map/all_gather | solution.py:23
  54.8 0.8 %collective-permute-done.2 = bf16[1,4,8,64]{3,2,1,0:T(8,128)(2,1)S(1)} collective-permute-done((bf16[1,4,8,64]{3,2,1,0:T(8,128)(2,1)S(1)}, bf16[1,4,8,64]{3,2,1,0:T(8,128)(2,1)S(1)}, u32[]{:S(2)}, u32[]{:S(2)}) %collective-permute-start.2) | collective-permute-done | bytes 4128 | tf_op jit(solution)/shard_map/ppermute | solution.py:22
  55.6 10.6 %all-gather.4 = bf16[12,4,8,64]{3,2,1,0:T(8,128)(2,1)S(1)} all-gather(bf16[3,4,8,64]{3,2,1,0:T(8,128)(2,1)S(1)} %pad_maximum_fusion), channel_id=6, replica_groups=mesh['gz'=128,'gy'=4] {'gy'}, dimensions={0}, use_global_device_ids=true | all-gather | bytes 61440 | tf_op jit(solution)/shard_map/all_gather | solution.py:152
  66.2 0.0 copy-done
  66.2 0.0 copy-done.2
  66.2 1.0 %shard_map.97 = bf16[1,4,8,128]{3,2,1,0:T(8,128)(2,1)} custom-call(bf16[4,3,4,8,64]{4,3,2,1,0:T(8,128)(2,1)S(1)} %bitcast.9, bf16[3,3,3,256,128]{4,3,2,1,0:T(8,128)(2,1)S(1)} %copy-done, f32[1,128]{1,0:T(1,128)S(1)} %bitcast.12), custom_call_target="tpu_custom_call" | custom-call | flops 134217728 | bytes 1048576 | tf_op jit(solution)/shard_map/pallas_call | solution.py:37
  (3 shorter events, 0.1 us)
Async XLA Ops:
  1.6 17.8 %collective-permute-start = (bf16[3,4,32,128]{3,2,1,0:T(8,128)(2,1)S(1)}, bf16[3,4,32,128]{3,2,1,0:T(8,128)(2,1)S(1)}, u32[]{:S(2)}, u32[]{:S(2)}) collective-permute-start(bf16[3,4,32,128]{3,2,1,0:T(8,128)(2,1)S(1)} %get-tuple-element.17), channel_id=1, source_target_pairs={{4,8},{12,16},{20,24},{28,32},{36,40},{44,48},{52,56},{60,64},{68,... | collective-permute-start | bytes 294920 | tf_op jit(solution)/shard_map/ppermute | solution.py:22
  19.4 0.9 %copy-start.1 = (bf16[4,4,32,128]{3,2,1,0:T(8,128)(2,1)S(1)}, bf16[4,4,32,128]{3,2,1,0:T(8,128)(2,1)}, u32[]{:S(2)}) copy-start(bf16[4,4,32,128]{3,2,1,0:T(8,128)(2,1)} %volume.1) | copy-start | bytes 393220
  20.4 5.6 %collective-permute-start.1 = (bf16[10,32,128]{2,1,0:T(8,128)(2,1)S(1)}, bf16[10,32,128]{2,1,0:T(8,128)(2,1)S(1)}, u32[]{:S(2)}, u32[]{:S(2)}) collective-permute-start(bf16[10,32,128]{2,1,0:T(8,128)(2,1)S(1)} %get-tuple-element.12), channel_id=1, source_target_pairs={{1,2},{2,1},{5,6},{6,5},{9,10},{10,9},{13,14},{14,13},{17,18},{18,... | collective-permute-start | bytes 245768 | tf_op jit(solution)/shard_map/ppermute | solution.py:22
  26.0 1.2 %copy-start.3 = (bf16[3,3,3,128,128]{4,3,2,1,0:T(8,128)(2,1)S(1)}, bf16[3,3,3,128,128]{4,3,2,1,0:T(8,128)(2,1)}, u32[]{:S(2)}) copy-start(bf16[3,3,3,128,128]{4,3,2,1,0:T(8,128)(2,1)} %kernel.2) | copy-start | bytes 2654212
  27.2 0.7 copy-start.5
  27.8 18.1 %copy-start.4 = (bf16[3,3,3,128,64]{3,4,2,1,0:T(8,128)(2,1)S(1)}, bf16[3,3,3,128,64]{3,4,2,1,0:T(8,128)(2,1)}, u32[]{:S(2)}) copy-start(bf16[3,3,3,128,64]{3,4,2,1,0:T(8,128)(2,1)} %param.10) | copy-start | bytes 1327108
  27.8 18.1 %copy-start.6 = (f32[64]{0:T(128)S(1)}, f32[64]{0:T(128)}, u32[]{:S(2)}) copy-start(f32[64]{0:T(128)} %param.11) | copy-start | bytes 772
  27.8 38.4 %copy-start = (bf16[3,3,3,256,128]{4,3,2,1,0:T(8,128)(2,1)S(1)}, bf16[3,3,3,256,128]{4,3,2,1,0:T(8,128)(2,1)}, u32[]{:S(2)}) copy-start(bf16[3,3,3,256,128]{4,3,2,1,0:T(8,128)(2,1)} %kernel.3) | copy-start | bytes 5308420
  27.8 38.4 %copy-start.2 = (f32[128]{0:T(128)S(1)}, f32[128]{0:T(128)}, u32[]{:S(2)}) copy-start(f32[128]{0:T(128)} %param.13) | copy-start | bytes 1540
  47.0 8.6 %collective-permute-start.2 = (bf16[1,4,8,64]{3,2,1,0:T(8,128)(2,1)S(1)}, bf16[1,4,8,64]{3,2,1,0:T(8,128)(2,1)S(1)}, u32[]{:S(2)}, u32[]{:S(2)}) collective-permute-start(bf16[1,4,8,64]{3,2,1,0:T(8,128)(2,1)S(1)} %get-tuple-element.16), channel_id=1, source_target_pairs={{4,8},{12,16},{20,24},{28,32},{36,40},{44,48},{52,56},{60,64},{68,... | collective-permute-start | bytes 12296 | tf_op jit(solution)/shard_map/ppermute | solution.py:22

commit v2 on v1

v2 whole, which is shorter than its diff:
```python
import jax
import jax.numpy as jnp
from jax import lax
from jax.experimental import pallas as pl
from jax.experimental.pallas import tpu as pltpu
from jax.sharding import PartitionSpec as P

BF16, F32 = jnp.bfloat16, jnp.float32


def even_groups(peers):
    return [[i, i + 1] for i in range(0, peers, 2)]


def odd_pairs(peers):
    pairs = [(i, i + 1) for i in range(1, peers - 1, 2)]
    return pairs + [(j, i) for i, j in pairs]


def swap(outward, inward, axis):
    peers = lax.axis_size(axis)
    across = lax.ppermute(outward, axis, odd_pairs(peers))
    pair = lax.all_gather(inward, axis, axis_index_groups=even_groups(peers))
    return pair, across


def local(body, inputs, outs, scratch=(), flops=0, kept=(), sems=0):
    vmem, kept_in_place = pl.BlockSpec(memory_space=pltpu.VMEM), pl.BlockSpec(memory_space=pltpu.HBM)
    specs = [kept_in_place if n in kept else vmem for n in range(len(inputs) + len(outs))]
    inputs = [pltpu.with_memory_space_constraint(a, pltpu.HBM) if n in kept else a for n, a in enumerate(inputs)]
    return pl.pallas_call(
        body,
        out_shape=[jax.ShapeDtypeStruct(*out) for out in outs],
        in_specs=specs[: len(inputs)],
        out_specs=specs[len(inputs) :],
        scratch_shapes=[pltpu.VMEM(*one) for one in scratch] + [pltpu.SemaphoreType.DMA((sems,))] * (sems > 0),
        cost_estimate=pl.CostEstimate(flops=flops, bytes_accessed=1 << 20, transcendentals=0),
        compiler_params=pltpu.CompilerParams(vmem_limit_bytes=32 << 20),
    )(*inputs)


def three_taps(wide, width, chans):
    cells = wide.shape[0]
    column = lax.broadcasted_iota(jnp.int32, (cells, chans), 0) % width
    left = jnp.where(column == 0, 0.0, pltpu.roll(wide[:, :chans], 1, 0))
    right = jnp.where(column == width - 1, 0.0, pltpu.roll(wide[:, 2 * chans :], cells - 1, 0))
    return left + wide[:, chans : 2 * chans] + right


TAPS = [(i, j) for i in range(3) for j in range(3)]


def edges(volume, own, outward, inward, sem):
    odd = lax.axis_index("gz") % 2
    read = pltpu.make_async_copy(volume, own, sem.at[0])
    read.start()
    read.wait()
    outward[...] = own[pl.ds(odd, 3)]
    inward[...] = own[pl.ds(1 - odd, 3)]


def fetch(kernel, bias, weights, offset, sem):
    reads = [pltpu.make_async_copy(bias, offset, sem.at[27])]
    for n, (i, j) in enumerate(TAPS):
        for tap in range(3):
            block = weights.at[128 * n : 128 * n + 128, 128 * tap : 128 * tap + 128]
            reads.append(pltpu.make_async_copy(kernel.at[i, j, tap], block, sem.at[3 * n + tap]))
    for read in reads:
        read.start()
    for read in reads:
        read.wait()


def join(volume, pair, across, wide, rows):
    odd, gy = lax.axis_index("gz") % 2, lax.axis_index("gy")
    wide[3:7] = volume[...]
    wide[pl.ds(7 * (1 - odd), 3)] = pair[1 - odd]
    wide[pl.ds(7 * odd, 3)] = across[...]
    rows[0] = wide[:, 3 * (1 - gy % 2)]
    rows[1] = wide[:, jnp.where(gy < 2, 2, 1)]


def level_a(wide, rows, weights, bias, skip, ship, x, most):
    gy = lax.axis_index("gy")
    core = gy % 2
    x[:, 1:5] = wide[...]
    x[:, 5 * (1 - core)] = rows[1 - core, 0]
    x[:, 5 * core] = jnp.zeros((10, 32, 128), BF16)
    open_row = jnp.where(gy == 1, 3, jnp.where(gy == 2, 0, 4))
    row = lax.broadcasted_iota(jnp.int32, (256, 128), 0) // 32 % 4
    for p in (1, 2, 0, 3):
        z = 2 * p
        cells = jnp.concatenate([x[z + i : z + i + 2, j : j + 4].reshape(256, 128) for i, j in TAPS], axis=1)
        sums = jnp.dot(cells, weights[...], preferred_element_type=F32)
        out = jnp.maximum(three_taps(sums, 32, 128) + bias[...], 0.0)
        if p in (1, 2):
            skip[z - 2 : z] = out.astype(BF16).reshape(2, 4, 32, 128)
        closed = jnp.where(row == open_row, 0.0, out)
        most[...] = jnp.max(closed.reshape(2, 2, 2, 32, 128), axis=(0, 2)).reshape(64, 128)
        small = jnp.maximum(most[pl.ds(0, 32, stride=2)], most[pl.ds(1, 32, stride=2)])
        ship[p] = small.astype(BF16)

    @pl.when((gy == 1) | (gy == 2))
    def _():
        ship[4:14] = wide[:, jnp.where(gy == 1, 3, 0)]

    @pl.when((gy == 0) | (gy == 3))
    def _():
        ship[4:14] = rows[1 - core, 1]


def level_b(ships, weights_a, bias_a, kernel, bias, patch, skip, pooled, x, most_a, most):
    gz, gy = lax.axis_index("gz"), lax.axis_index("gy")
    x[:, 0] = jnp.zeros((4, 16, 128), BF16)
    x[:, 9] = jnp.zeros((4, 16, 128), BF16)
    for g in range(4):
        x[:, 2 * g + 1 : 2 * g + 3] = ships[g, 0:4].reshape(4, 2, 16, 128)
    for r in range(2):
        cells = jnp.concatenate([ships[r + j, 4 + i : 12 + i].reshape(256, 128) for i, j in TAPS], axis=1)
        sums = jnp.dot(cells, weights_a[...], preferred_element_type=F32)
        out = jnp.maximum(three_taps(sums, 32, 128) + bias_a[...], 0.0)

        @pl.when(gy == r + 1)
        def _():
            patch[...] = out[64:192].astype(BF16).reshape(4, 32, 128)

        most_a[...] = jnp.max(out.reshape(4, 2, 32, 128), axis=1).reshape(128, 128)
        small = jnp.maximum(most_a[pl.ds(0, 64, stride=2)], most_a[pl.ds(1, 64, stride=2)])
        x[:, 4 + r] = jnp.maximum(x[:, 4 + r], small.astype(BF16).reshape(4, 16, 128))

    @pl.when(gz == 0)
    def _():
        x[0] = jnp.zeros((10, 16, 128), BF16)

    @pl.when(gz == lax.axis_size("gz") - 1)
    def _():
        x[3] = jnp.zeros((10, 16, 128), BF16)

    weights = jnp.concatenate(
        [jnp.concatenate([kernel[i, j, tap] for tap in range(3)], axis=0) for i, j in TAPS], axis=1
    )
    cells = jnp.concatenate([x[i : i + 2, j : j + 8].reshape(256, 128) for i, j in TAPS], axis=1)
    sums = lax.dot_general(cells, weights, (((1,), (1,)), ((), ())), preferred_element_type=F32)
    out = jnp.maximum(three_taps(sums, 16, 64) + bias[...], 0.0)
    skip[...] = out.astype(BF16).reshape(2, 8, 16, 64)
    most[...] = jnp.max(out.reshape(2, 4, 2, 16, 64), axis=(0, 2)).reshape(64, 64)
    small = jnp.maximum(most[pl.ds(0, 32, stride=2)], most[pl.ds(1, 32, stride=2)])
    pooled[...] = small.astype(BF16).reshape(1, 4, 8, 64)


def level_c(shards, kernel, bias, skip_a, patch, skip_b, bottom, out_a, out_b, x, whole, sem):
    gy = lax.axis_index("gy")
    write_b = pltpu.make_async_copy(skip_b, out_b, sem.at[1])
    write_b.start()
    whole[...] = skip_a[...]

    @pl.when(gy == 1)
    def _():
        whole[:, 3] = patch[...]

    @pl.when(gy == 2)
    def _():
        whole[:, 0] = patch[...]

    write_a = pltpu.make_async_copy(whole, out_a, sem.at[0])
    write_a.start()
    x[:, 0] = jnp.zeros((3, 8, 256), BF16)
    x[:, 5] = jnp.zeros((3, 8, 256), BF16)
    x[:, 1:5] = jnp.concatenate([shards[g] for g in range(4)], axis=-1)
    weights = jnp.concatenate(
        [jnp.concatenate([kernel[i, j, tap] for tap in range(3)], axis=1) for i, j in TAPS], axis=0
    )
    cells = jnp.concatenate([x[i, j : j + 4].reshape(32, 256) for i, j in TAPS], axis=1)
    sums = jnp.dot(cells, weights, preferred_element_type=F32)
    out = jnp.maximum(three_taps(sums, 8, 128) + bias[...], 0.0)
    bottom[...] = out.astype(BF16).reshape(1, 4, 8, 128)
    write_a.wait()
    write_b.wait()


def levels(volume, kernel_a, bias_a, kernel_b, bias_b, kernel_c, bias_c):
    slab = ((3, 4, 32, 128), BF16)
    own, outward, inward = local(edges, (volume,), [((4, 4, 32, 128), BF16), slab, slab], kept=(0,), sems=1)
    pair, across = swap(outward, inward, "gz")
    weights, offset = local(
        fetch, (kernel_a, bias_a[None]), [((1152, 384), BF16), ((1, 128), F32)], kept=(0, 1), sems=28
    )
    wide, rows = local(join, (own, pair, across), [((10, 4, 32, 128), BF16), ((2, 10, 32, 128), BF16)])
    rows = lax.all_gather(rows, "gy", axis_index_groups=even_groups(4))
    skip_a, ship = local(
        level_a,
        (wide, rows, weights, offset),
        [((4, 4, 32, 128), BF16), ((14, 32, 128), BF16)],
        [((10, 6, 32, 128), BF16), ((64, 128), F32)],
        1 << 30,
    )
    patch, skip_b, pooled_b = local(
        level_b,
        (lax.all_gather(ship, "gy"), weights, offset, jnp.swapaxes(kernel_b, 3, 4), bias_b[None]),
        [((4, 32, 128), BF16), ((2, 8, 16, 64), BF16), ((1, 4, 8, 64), BF16)],
        [((4, 10, 16, 128), BF16), ((128, 128), F32), ((64, 64), F32)],
        1 << 29,
    )
    pair, across = swap(pooled_b, pooled_b, "gz")
    odd = lax.axis_index("gz") % 2
    partner = lax.dynamic_index_in_dim(pair, 1 - odd, 0, keepdims=False)
    deep = jnp.concatenate([jnp.where(odd == 1, partner, across), pooled_b, jnp.where(odd == 1, across, partner)])
    bottom, skip_a, skip_b = local(
        level_c,
        (lax.all_gather(deep, "gy"), kernel_c, bias_c[None], skip_a, patch, skip_b),
        [((1, 4, 8, 128), BF16), ((4, 4, 32, 128), BF16), ((2, 8, 16, 64), BF16)],
        [((3, 6, 8, 256), BF16), ((4, 4, 32, 128), BF16)],
        1 << 27,
        kept=(7, 8),
        sems=2,
    )
    return (skip_a, skip_b, bottom)


def solution(mesh):
    return jax.shard_map(
        levels,
        mesh=mesh,
        in_specs=(
            P("gz", "gy", None, None),
            P(),
            P(),
            P(None, None, None, None, "gy"),
            P("gy"),
            P(None, None, None, None, "gy"),
            P("gy"),
        ),
        out_specs=(P("gz", "gy", None, None), P("gz", None, None, "gy"), P("gz", None, None, "gy")),
        check_vma=False,
    )
```

time: 67.5 us -> 62.2 us (0.921)
  the two profiles are of different devices: /device:TPU:57 before, /device:TPU:41 now
where the time goes in v2:
time: 62.2 us; the launch traced here: 61.9 us
  blocking collectives  34.9 us (56%)
  starting transfers between devices  15.6 us (25%)
  Pallas kernels  7.22 us (12%)
  waiting for transfers between devices  3.46 us (6%)
  between operations  0.72 us (1%)
    ppermute x2, starting transfers between devices, swap(): across = lax.ppermute(outward, axis, odd_pairs(peers))  15.6 us
    all_gather x1, blocking collectives, levels(): lax.all_gather(ship, 'gy')  13.4 us
    all_gather x1, blocking collectives, levels(): lax.all_gather(deep, 'gy')  10.4 us
    all_gather x2, blocking collectives, swap(): pair = lax.all_gather(inward, axis, axis_index_groups=even_groups(peers))  7.34 us
    pallas_call x6, Pallas kernels, local(): pl.pallas_call(body, out_shape=[jax.ShapeDtypeStruct(*out) for out in out...  7.22 us
    all_gather x1, blocking collectives, levels(): rows = lax.all_gather(rows, 'gy', axis_index_groups=even_groups(4))  3.78 us
    ppermute x2, waiting for transfers between devices, swap(): across = lax.ppermute(outward, axis, odd_pairs(peers))  3.46 us
  transfers between devices with their start and end apart: 2, of which 1 were waited for; matrix products, arithmetic and copies ran while one was open for 0% of the time, Pallas kernels for 2%

profile of v2, /device:TPU:41, one launch (start us, length us, event | category | flops | bytes accessed | tf_op | source)
XLA Modules:
  0.0 61.9 jit_solution(12127455612934889493)
XLA Ops:
  0.6 0.9 %shard_map.94 = (bf16[4,4,32,128]{3,2,1,0:T(8,128)(2,1)S(1)}, bf16[3,4,32,128]{3,2,1,0:T(8,128)(2,1)S(1)}, bf16[3,4,32,128]{3,2,1,0:T(8,128)(2,1)S(1)}) custom-call(bf16[4,4,32,128]{3,2,1,0:T(8,128)(2,1)} %volume.1), custom_call_target="tpu_custom_call" | custom-call | bytes 1048576 | tf_op jit(solution)/shard_map/pallas_call | solution.py:31
  1.6 13.6 %collective-permute-start = (bf16[3,4,32,128]{3,2,1,0:T(8,128)(2,1)S(1)}, bf16[3,4,32,128]{3,2,1,0:T(8,128)(2,1)S(1)}, u32[]{:S(2)}, u32[]{:S(2)}) collective-permute-start(bf16[3,4,32,128]{3,2,1,0:T(8,128)(2,1)S(1)} %get-tuple-element.20), channel_id=1, source_target_pairs={{4,8},{12,16},{20,24},{28,32},{36,40},{44,48},{52,56},{60,64},{68,... | collective-permute-start | bytes 294920 | tf_op jit(solution)/shard_map/ppermute | solution.py:22
  15.2 1.4 %shard_map.96 = (bf16[1152,384]{1,0:T(8,128)(2,1)S(1)}, f32[1,128]{1,0:T(1,128)S(1)}) custom-call(bf16[3,3,3,128,128]{4,3,2,1,0:T(8,128)(2,1)} %kernel.2, f32[1,128]{1,0:T(1,128)} %bitcast.15), custom_call_target="tpu_custom_call" | custom-call | bytes 1048576 | tf_op jit(solution)/shard_map/pallas_call | solution.py:31
  16.6 4.1 %all-gather = bf16[6,4,32,128]{3,2,1,0:T(8,128)(2,1)S(1)} all-gather(bf16[3,4,32,128]{3,2,1,0:T(8,128)(2,1)S(1)} %get-tuple-element.19), channel_id=2, replica_groups={{0,4},{8,12},{16,20},{24,28},{32,36},{40,44},{48,52},{56,60},{64,68},{7..., dimensions={0}, use_global_device_ids=true | all-gather | bytes 294912 | tf_op jit(solution)/shard_map/all_gather | solution.py:23
  20.7 0.0 collective-permute-done.across
  20.8 3.8 %all-gather.1 = bf16[4,10,32,128]{3,2,1,0:T(8,128)(2,1)S(1)} all-gather(bf16[2,10,32,128]{3,2,1,0:T(8,128)(2,1)S(1)} %get-tuple-element.22), channel_id=3, replica_groups={{0,1},{2,3},{4,5},{6,7},{8,9},{10,11},{12,13},{14,15},{16,17},{18,19},{..., dimensions={0}, use_global_device_ids=true | all-gather | bytes 491520 | tf_op jit(solution)/shard_map/all_gather | solution.py:189
  24.6 0.0 copy-start.2
  24.6 0.0 copy-start.3
  24.6 1.5 %shard_map.97 = (bf16[4,4,32,128]{3,2,1,0:T(8,128)(2,1)S(1)}, bf16[14,32,128]{2,1,0:T(8,128)(2,1)S(1)}) custom-call(bf16[10,4,32,128]{3,2,1,0:T(8,128)(2,1)S(1)} %get-tuple-element.21.wide, bf16[2,2,10,32,128]{4,3,2,1,0:T(8,128)(2,1)S(1)} %bitcast.11, bf16[1152,384]{1,0:T(8,128)(2,1)S(1)} %get-tuple-element.23.weights.weights_a, ...), custom_call_target="tpu_custom_call" | custom-call | flops 1073741824 | bytes 1048576 | tf_op jit(solution)/shard_map/pallas_call | solution.py:31
  26.1 0.0 copy-start
  26.1 0.0 copy-start.1
  26.1 13.4 %all-gather.2 = bf16[56,32,128]{2,1,0:T(8,128)(2,1)S(1)} all-gather(bf16[14,32,128]{2,1,0:T(8,128)(2,1)S(1)} %get-tuple-element.25), channel_id=4, replica_groups=mesh['gz'=128,'gy'=4] {'gy'}, dimensions={0}, use_global_device_ids=true | all-gather | bytes 573440 | tf_op jit(solution)/shard_map/all_gather | solution.py:199
  39.5 0.0 copy-done.2
  39.5 0.0 copy-done.3
  39.5 1.8 %shard_map.98 = (bf16[4,32,128]{2,1,0:T(8,128)(2,1)S(1)}, bf16[2,8,16,64]{3,2,1,0:T(8,128)(2,1)S(1)}, bf16[1,4,8,64]{3,2,1,0:T(8,128)(2,1)S(1)}) custom-call(bf16[4,14,32,128]{3,2,1,0:T(8,128)(2,1)S(1)} %bitcast.9, bf16[1152,384]{1,0:T(8,128)(2,1)S(1)} %get-tuple-element.23.weights.weights_a, f32[1,128]{1,0:T(1,128)S(1)} %get-tuple-element.24.bias.bias_a, ...), custom_call_target="tpu_custom_call" | custom-call | flops 536870912 | bytes 1048576 | tf_op jit(solution)/shard_map/pallas_call | solution.py:31
  41.3 1.9 %collective-permute-start.1 = (bf16[1,4,8,64]{3,2,1,0:T(8,128)(2,1)S(1)}, bf16[1,4,8,64]{3,2,1,0:T(8,128)(2,1)S(1)}, u32[]{:S(2)}, u32[]{:S(2)}) collective-permute-start(bf16[1,4,8,64]{3,2,1,0:T(8,128)(2,1)S(1)} %get-tuple-element.26), channel_id=1, source_target_pairs={{4,8},{12,16},{20,24},{28,32},{36,40},{44,48},{52,56},{60,64},{68,... | collective-permute-start | bytes 12296 | tf_op jit(solution)/shard_map/ppermute | solution.py:22
  43.3 3.2 %all-gather.3 = bf16[2,4,8,64]{3,2,1,0:T(8,128)(2,1)S(1)} all-gather(bf16[1,4,8,64]{3,2,1,0:T(8,128)(2,1)S(1)} %get-tuple-element.26), channel_id=5, replica_groups={{0,4},{8,12},{16,20},{24,28},{32,36},{40,44},{48,52},{56,60},{64,68},{7..., dimensions={0}, use_global_device_ids=true | all-gather | bytes 12288 | tf_op jit(solution)/shard_map/all_gather | solution.py:23
  46.5 3.5 %collective-permute-done.1 = bf16[1,4,8,64]{3,2,1,0:T(8,128)(2,1)S(1)} collective-permute-done((bf16[1,4,8,64]{3,2,1,0:T(8,128)(2,1)S(1)}, bf16[1,4,8,64]{3,2,1,0:T(8,128)(2,1)S(1)}, u32[]{:S(2)}, u32[]{:S(2)}) %collective-permute-start.1) | collective-permute-done | bytes 4128 | tf_op jit(solution)/shard_map/ppermute | solution.py:22
  50.0 10.4 %all-gather.4 = bf16[12,4,8,64]{3,2,1,0:T(8,128)(2,1)S(1)} all-gather(bf16[3,4,8,64]{3,2,1,0:T(8,128)(2,1)S(1)} %pad_maximum_fusion), channel_id=6, replica_groups=mesh['gz'=128,'gy'=4] {'gy'}, dimensions={0}, use_global_device_ids=true | all-gather | bytes 61440 | tf_op jit(solution)/shard_map/all_gather | solution.py:210
  60.4 0.0 copy-done
  60.4 0.0 copy-done.1
  60.4 1.6 %shard_map.99 = (bf16[1,4,8,128]{3,2,1,0:T(8,128)(2,1)}, bf16[4,4,32,128]{3,2,1,0:T(8,128)(2,1)}, bf16[2,8,16,64]{3,2,1,0:T(8,128)(2,1)}) custom-call(bf16[4,3,4,8,64]{4,3,2,1,0:T(8,128)(2,1)S(1)} %bitcast.10, bf16[3,3,3,256,128]{4,3,2,1,0:T(8,128)(2,1)S(1)} %copy-done, f32[1,128]{1,0:T(1,128)S(1)} %bitcast.12, ...), custom_call_target="tpu_custom_call" | custom-call | flops 134217728 | bytes 1048576 | tf_op jit(solution)/shard_map/pallas_call | solution.py:31
  (3 shorter events, 0.1 us)
Async XLA Ops:
  1.6 19.2 %collective-permute-start = (bf16[3,4,32,128]{3,2,1,0:T(8,128)(2,1)S(1)}, bf16[3,4,32,128]{3,2,1,0:T(8,128)(2,1)S(1)}, u32[]{:S(2)}, u32[]{:S(2)}) collective-permute-start(bf16[3,4,32,128]{3,2,1,0:T(8,128)(2,1)S(1)} %get-tuple-element.20), channel_id=1, source_target_pairs={{4,8},{12,16},{20,24},{28,32},{36,40},{44,48},{52,56},{60,64},{68,... | collective-permute-start | bytes 294920 | tf_op jit(solution)/shard_map/ppermute | solution.py:22
  24.6 15.0 %copy-start.2 = (bf16[3,3,3,128,64]{3,4,2,1,0:T(8,128)(2,1)S(1)}, bf16[3,3,3,128,64]{3,4,2,1,0:T(8,128)(2,1)}, u32[]{:S(2)}) copy-start(bf16[3,3,3,128,64]{3,4,2,1,0:T(8,128)(2,1)} %param.10) | copy-start | bytes 1327108
  24.6 15.0 %copy-start.3 = (f32[64]{0:T(128)S(1)}, f32[64]{0:T(128)}, u32[]{:S(2)}) copy-start(f32[64]{0:T(128)} %param.11) | copy-start | bytes 772
  26.1 34.3 %copy-start = (bf16[3,3,3,256,128]{4,3,2,1,0:T(8,128)(2,1)S(1)}, bf16[3,3,3,256,128]{4,3,2,1,0:T(8,128)(2,1)}, u32[]{:S(2)}) copy-start(bf16[3,3,3,256,128]{4,3,2,1,0:T(8,128)(2,1)} %kernel.3) | copy-start | bytes 5308420
  26.1 34.3 %copy-start.1 = (f32[128]{0:T(128)S(1)}, f32[128]{0:T(128)}, u32[]{:S(2)}) copy-start(f32[128]{0:T(128)} %param.13) | copy-start | bytes 1540
  41.3 8.6 %collective-permute-start.1 = (bf16[1,4,8,64]{3,2,1,0:T(8,128)(2,1)S(1)}, bf16[1,4,8,64]{3,2,1,0:T(8,128)(2,1)S(1)}, u32[]{:S(2)}, u32[]{:S(2)}) collective-permute-start(bf16[1,4,8,64]{3,2,1,0:T(8,128)(2,1)S(1)} %get-tuple-element.26), channel_id=1, source_target_pairs={{4,8},{12,16},{20,24},{28,32},{36,40},{44,48},{52,56},{60,64},{68,... | collective-permute-start | bytes 12296 | tf_op jit(solution)/shard_map/ppermute | solution.py:22

commit v3 on v2

--- a/solution.py
+++ b/solution.py
@@ -12,19 +12,16 @@
     return [[i, i + 1] for i in range(0, peers, 2)]
 
 
-def odd_pairs(peers):
-    pairs = [(i, i + 1) for i in range(1, peers - 1, 2)]
-    return pairs + [(j, i) for i, j in pairs]
-
-
 def swap(outward, inward, axis):
     peers = lax.axis_size(axis)
-    across = lax.ppermute(outward, axis, odd_pairs(peers))
-    pair = lax.all_gather(inward, axis, axis_index_groups=even_groups(peers))
+    even = [(i, i ^ 1) for i in range(peers)]
+    odd = [(i, i + 1) for i in range(1, peers - 1, 2)]
+    across = lax.ppermute(outward, axis, odd + [(j, i) for i, j in odd])
+    pair = lax.ppermute(inward, axis, even)
     return pair, across
 
 
-def local(body, inputs, outs, scratch=(), flops=0, kept=(), sems=0):
+def local(body, inputs, outs, scratch=(), flops=0, kept=(), sems=0, same={}):
     vmem, kept_in_place = pl.BlockSpec(memory_space=pltpu.VMEM), pl.BlockSpec(memory_space=pltpu.HBM)
     specs = [kept_in_place if n in kept else vmem for n in range(len(inputs) + len(outs))]
     inputs = [pltpu.with_memory_space_constraint(a, pltpu.HBM) if n in kept else a for n, a in enumerate(inputs)]
@@ -33,6 +30,7 @@
         out_shape=[jax.ShapeDtypeStruct(*out) for out in outs],
         in_specs=specs[: len(inputs)],
         out_specs=specs[len(inputs) :],
+        input_output_aliases=same,
         scratch_shapes=[pltpu.VMEM(*one) for one in scratch] + [pltpu.SemaphoreType.DMA((sems,))] * (sems > 0),
         cost_estimate=pl.CostEstimate(flops=flops, bytes_accessed=1 << 20, transcendentals=0),
         compiler_params=pltpu.CompilerParams(vmem_limit_bytes=32 << 20),
@@ -74,13 +72,13 @@
 def join(volume, pair, across, wide, rows):
     odd, gy = lax.axis_index("gz") % 2, lax.axis_index("gy")
     wide[3:7] = volume[...]
-    wide[pl.ds(7 * (1 - odd), 3)] = pair[1 - odd]
+    wide[pl.ds(7 * (1 - odd), 3)] = pair[...]
     wide[pl.ds(7 * odd, 3)] = across[...]
     rows[0] = wide[:, 3 * (1 - gy % 2)]
     rows[1] = wide[:, jnp.where(gy < 2, 2, 1)]
 
 
-def level_a(wide, rows, weights, bias, skip, ship, x, most):
+def level_a(wide, rows, weights, bias, skip, ship, x, most, own, sem):
     gy = lax.axis_index("gy")
     core = gy % 2
     x[:, 1:5] = wide[...]
@@ -94,7 +92,10 @@
         sums = jnp.dot(cells, weights[...], preferred_element_type=F32)
         out = jnp.maximum(three_taps(sums, 32, 128) + bias[...], 0.0)
         if p in (1, 2):
-            skip[z - 2 : z] = out.astype(BF16).reshape(2, 4, 32, 128)
+            own[z - 2 : z] = out.astype(BF16).reshape(2, 4, 32, 128)
+        if p == 2:
+            write = pltpu.make_async_copy(own, skip, sem.at[0])
+            write.start()
         closed = jnp.where(row == open_row, 0.0, out)
         most[...] = jnp.max(closed.reshape(2, 2, 2, 32, 128), axis=(0, 2)).reshape(64, 128)
         small = jnp.maximum(most[pl.ds(0, 32, stride=2)], most[pl.ds(1, 32, stride=2)])
@@ -107,6 +108,8 @@
     @pl.when((gy == 0) | (gy == 3))
     def _():
         ship[4:14] = rows[1 - core, 1]
+
+    write.wait()
 
 
 def level_b(ships, weights_a, bias_a, kernel, bias, patch, skip, pooled, x, most_a, most):
@@ -148,22 +151,17 @@
     pooled[...] = small.astype(BF16).reshape(1, 4, 8, 64)
 
 
-def level_c(shards, kernel, bias, skip_a, patch, skip_b, bottom, out_a, out_b, x, whole, sem):
+def level_c(shards, kernel, bias, skip_a, patch, skip_b, bottom, out_a, out_b, x, sem):
     gy = lax.axis_index("gy")
-    write_b = pltpu.make_async_copy(skip_b, out_b, sem.at[1])
+    write_b = pltpu.make_async_copy(skip_b, out_b, sem.at[0])
     write_b.start()
-    whole[...] = skip_a[...]
-
-    @pl.when(gy == 1)
-    def _():
-        whole[:, 3] = patch[...]
-
-    @pl.when(gy == 2)
-    def _():
-        whole[:, 0] = patch[...]
-
-    write_a = pltpu.make_async_copy(whole, out_a, sem.at[0])
-    write_a.start()
+    inner = (gy == 1) | (gy == 2)
+    write_a = pltpu.make_async_copy(patch, out_a.at[:, jnp.where(gy == 1, 3, 0)], sem.at[1])
+
+    @pl.when(inner)
+    def _():
+        write_a.start()
+
     x[:, 0] = jnp.zeros((3, 8, 256), BF16)
     x[:, 5] = jnp.zeros((3, 8, 256), BF16)
     x[:, 1:5] = jnp.concatenate([shards[g] for g in range(4)], axis=-1)
@@ -174,8 +172,11 @@
     sums = jnp.dot(cells, weights, preferred_element_type=F32)
     out = jnp.maximum(three_taps(sums, 8, 128) + bias[...], 0.0)
     bottom[...] = out.astype(BF16).reshape(1, 4, 8, 128)
-    write_a.wait()
     write_b.wait()
+
+    @pl.when(inner)
+    def _():
+        write_a.wait()
 
 
 def levels(volume, kernel_a, bias_a, kernel_b, bias_b, kernel_c, bias_c):
@@ -191,8 +192,10 @@
         level_a,
         (wide, rows, weights, offset),
         [((4, 4, 32, 128), BF16), ((14, 32, 128), BF16)],
-        [((10, 6, 32, 128), BF16), ((64, 128), F32)],
+        [((10, 6, 32, 128), BF16), ((64, 128), F32), ((4, 4, 32, 128), BF16)],
         1 << 30,
+        kept=(4,),
+        sems=1,
     )
     patch, skip_b, pooled_b = local(
         level_b,
@@ -203,16 +206,16 @@
     )
     pair, across = swap(pooled_b, pooled_b, "gz")
     odd = lax.axis_index("gz") % 2
-    partner = lax.dynamic_index_in_dim(pair, 1 - odd, 0, keepdims=False)
-    deep = jnp.concatenate([jnp.where(odd == 1, partner, across), pooled_b, jnp.where(odd == 1, across, partner)])
+    deep = jnp.concatenate([jnp.where(odd == 1, pair, across), pooled_b, jnp.where(odd == 1, across, pair)])
     bottom, skip_a, skip_b = local(
         level_c,
         (lax.all_gather(deep, "gy"), kernel_c, bias_c[None], skip_a, patch, skip_b),
         [((1, 4, 8, 128), BF16), ((4, 4, 32, 128), BF16), ((2, 8, 16, 64), BF16)],
-        [((3, 6, 8, 256), BF16), ((4, 4, 32, 128), BF16)],
+        [((3, 6, 8, 256), BF16)],
         1 << 27,
-        kept=(7, 8),
+        kept=(3, 7, 8),
         sems=2,
+        same={3: 1},
     )
     return (skip_a, skip_b, bottom)
 

time: 62.2 us -> 63.2 us (1.016)
  the two profiles are of different devices: /device:TPU:41 before, /device:TPU:57 now
where the time goes in v3:
time: 63.2 us; the launch traced here: 62.9 us
  starting transfers between devices  26.8 us (42%)
  blocking collectives  26.1 us (41%)
  Pallas kernels  7.59 us (12%)
  waiting for transfers between devices  1.61 us (3%)
  between operations  0.74 us (1%)
    ppermute x2, starting transfers between devices, swap(): across = lax.ppermute(outward, axis, odd + [(j, i) for i, j in odd])  21.8 us
    all_gather x1, blocking collectives, levels(): lax.all_gather(ship, 'gy')  12.5 us
    all_gather x1, blocking collectives, levels(): lax.all_gather(deep, 'gy')  10.1 us
    pallas_call x6, Pallas kernels, local(): pl.pallas_call(body, out_shape=[jax.ShapeDtypeStruct(*out) for out in out...  7.59 us
    ppermute x2, starting transfers between devices, swap(): pair = lax.ppermute(inward, axis, even)  5.04 us
    all_gather x1, blocking collectives, levels(): rows = lax.all_gather(rows, 'gy', axis_index_groups=even_groups(4))  3.5 us
    ppermute x2, waiting for transfers between devices, swap(): across = lax.ppermute(outward, axis, odd + [(j, i) for i, j in odd])  1.6 us
  transfers between devices with their start and end apart: 4, of which 2 were waited for; matrix products, arithmetic and copies ran while one was open for 0% of the time, Pallas kernels for 2%

profile of v3, /device:TPU:57, one launch (start us, length us, event | category | flops | bytes accessed | tf_op | source)
XLA Modules:
  0.0 62.9 jit_solution(9797657541295015867)
XLA Ops:
  0.6 0.9 %shard_map.94 = (bf16[4,4,32,128]{3,2,1,0:T(8,128)(2,1)S(1)}, bf16[3,4,32,128]{3,2,1,0:T(8,128)(2,1)S(1)}, bf16[3,4,32,128]{3,2,1,0:T(8,128)(2,1)S(1)}) custom-call(bf16[4,4,32,128]{3,2,1,0:T(8,128)(2,1)} %volume.1), custom_call_target="tpu_custom_call" | custom-call | bytes 1048576 | tf_op jit(solution)/shard_map/pallas_call | solution.py:28
  1.6 3.1 %collective-permute-start = (bf16[3,4,32,128]{3,2,1,0:T(8,128)(2,1)S(1)}, bf16[3,4,32,128]{3,2,1,0:T(8,128)(2,1)S(1)}, u32[]{:S(2)}, u32[]{:S(2)}) collective-permute-start(bf16[3,4,32,128]{3,2,1,0:T(8,128)(2,1)S(1)} %get-tuple-element.19), channel_id=1, source_target_pairs={{0,4},{4,0},{8,12},{12,8},{16,20},{20,16},{24,28},{28,24},{32,36},... | collective-permute-start | bytes 294920 | tf_op jit(solution)/shard_map/ppermute | solution.py:20
  4.7 13.0 %collective-permute-start.1 = (bf16[3,4,32,128]{3,2,1,0:T(8,128)(2,1)S(1)}, bf16[3,4,32,128]{3,2,1,0:T(8,128)(2,1)S(1)}, u32[]{:S(2)}, u32[]{:S(2)}) collective-permute-start(bf16[3,4,32,128]{3,2,1,0:T(8,128)(2,1)S(1)} %get-tuple-element.20), channel_id=1, source_target_pairs={{4,8},{12,16},{20,24},{28,32},{36,40},{44,48},{52,56},{60,64},{68,... | collective-permute-start | bytes 294920 | tf_op jit(solution)/shard_map/ppermute | solution.py:19
  17.7 1.4 %shard_map.96 = (bf16[1152,384]{1,0:T(8,128)(2,1)S(1)}, f32[1,128]{1,0:T(1,128)S(1)}) custom-call(bf16[3,3,3,128,128]{4,3,2,1,0:T(8,128)(2,1)} %kernel.2, f32[1,128]{1,0:T(1,128)} %bitcast.13), custom_call_target="tpu_custom_call" | custom-call | bytes 1048576 | tf_op jit(solution)/shard_map/pallas_call | solution.py:28
  19.1 0.0 collective-permute-done.pair
  19.1 0.6 collective-permute-done.1.across
  19.7 3.5 %all-gather = bf16[4,10,32,128]{3,2,1,0:T(8,128)(2,1)S(1)} all-gather(bf16[2,10,32,128]{3,2,1,0:T(8,128)(2,1)S(1)} %get-tuple-element.22), channel_id=2, replica_groups={{0,1},{2,3},{4,5},{6,7},{8,9},{10,11},{12,13},{14,15},{16,17},{18,19},{..., dimensions={0}, use_global_device_ids=true | all-gather | bytes 491520 | tf_op jit(solution)/shard_map/all_gather | solution.py:190
  23.2 0.0 copy-start.2
  23.2 0.0 copy-start.3
  23.2 2.0 %shard_map.97 = (bf16[4,4,32,128]{3,2,1,0:T(8,128)(2,1)}, bf16[14,32,128]{2,1,0:T(8,128)(2,1)S(1)}) custom-call(bf16[10,4,32,128]{3,2,1,0:T(8,128)(2,1)S(1)} %get-tuple-element.21.wide, bf16[2,2,10,32,128]{4,3,2,1,0:T(8,128)(2,1)S(1)} %bitcast.9, bf16[1152,384]{1,0:T(8,128)(2,1)S(1)} %get-tuple-element.23.weights.weights_a, ...), custom_call_target="tpu_custom_call" | custom-call | flops 1073741824 | bytes 1048576 | tf_op jit(solution)/shard_map/pallas_call | solution.py:28
  25.2 0.0 copy-start
  25.2 0.0 copy-start.1
  25.2 12.5 %all-gather.1 = bf16[56,32,128]{2,1,0:T(8,128)(2,1)S(1)} all-gather(bf16[14,32,128]{2,1,0:T(8,128)(2,1)S(1)} %get-tuple-element.25), channel_id=3, replica_groups=mesh['gz'=128,'gy'=4] {'gy'}, dimensions={0}, use_global_device_ids=true | all-gather | bytes 573440 | tf_op jit(solution)/shard_map/all_gather | solution.py:202
  37.7 0.0 copy-done.2
  37.7 0.0 copy-done.3
  37.7 1.8 %shard_map.98 = (bf16[4,32,128]{2,1,0:T(8,128)(2,1)S(1)}, bf16[2,8,16,64]{3,2,1,0:T(8,128)(2,1)S(1)}, bf16[1,4,8,64]{3,2,1,0:T(8,128)(2,1)S(1)}) custom-call(bf16[4,14,32,128]{3,2,1,0:T(8,128)(2,1)S(1)} %bitcast.7, bf16[1152,384]{1,0:T(8,128)(2,1)S(1)} %get-tuple-element.23.weights.weights_a, f32[1,128]{1,0:T(1,128)S(1)} %get-tuple-element.24.bias.bias_a, ...), custom_call_target="tpu_custom_call" | custom-call | flops 536870912 | bytes 1048576 | tf_op jit(solution)/shard_map/pallas_call | solution.py:28
  39.5 1.9 %collective-permute-start.2 = (bf16[1,4,8,64]{3,2,1,0:T(8,128)(2,1)S(1)}, bf16[1,4,8,64]{3,2,1,0:T(8,128)(2,1)S(1)}, u32[]{:S(2)}, u32[]{:S(2)}) collective-permute-start(bf16[1,4,8,64]{3,2,1,0:T(8,128)(2,1)S(1)} %get-tuple-element.26), channel_id=1, source_target_pairs={{0,4},{4,0},{8,12},{12,8},{16,20},{20,16},{24,28},{28,24},{32,36},... | collective-permute-start | bytes 12296 | tf_op jit(solution)/shard_map/ppermute | solution.py:20
  41.4 8.8 %collective-permute-start.3 = (bf16[1,4,8,64]{3,2,1,0:T(8,128)(2,1)S(1)}, bf16[1,4,8,64]{3,2,1,0:T(8,128)(2,1)S(1)}, u32[]{:S(2)}, u32[]{:S(2)}) collective-permute-start(bf16[1,4,8,64]{3,2,1,0:T(8,128)(2,1)S(1)} %get-tuple-element.26), channel_id=1, source_target_pairs={{4,8},{12,16},{20,24},{28,32},{36,40},{44,48},{52,56},{60,64},{68,... | collective-permute-start | bytes 12296 | tf_op jit(solution)/shard_map/ppermute | solution.py:19
  50.2 0.0 collective-permute-done.2
  50.2 1.0 %collective-permute-done.3 = bf16[1,4,8,64]{3,2,1,0:T(8,128)(2,1)S(1)} collective-permute-done((bf16[1,4,8,64]{3,2,1,0:T(8,128)(2,1)S(1)}, bf16[1,4,8,64]{3,2,1,0:T(8,128)(2,1)S(1)}, u32[]{:S(2)}, u32[]{:S(2)}) %collective-permute-start.3) | collective-permute-done | bytes 4128 | tf_op jit(solution)/shard_map/ppermute | solution.py:19
  51.3 10.1 %all-gather.2 = bf16[12,4,8,64]{3,2,1,0:T(8,128)(2,1)S(1)} all-gather(bf16[3,4,8,64]{3,2,1,0:T(8,128)(2,1)S(1)} %pad_maximum_fusion), channel_id=4, replica_groups=mesh['gz'=128,'gy'=4] {'gy'}, dimensions={0}, use_global_device_ids=true | all-gather | bytes 61440 | tf_op jit(solution)/shard_map/all_gather | solution.py:212
  61.4 0.0 copy-done
  61.4 0.0 copy-done.1
  61.4 1.5 %shard_map.99 = (bf16[1,4,8,128]{3,2,1,0:T(8,128)(2,1)}, bf16[4,4,32,128]{3,2,1,0:T(8,128)(2,1)}, bf16[2,8,16,64]{3,2,1,0:T(8,128)(2,1)}) custom-call(bf16[4,3,4,8,64]{4,3,2,1,0:T(8,128)(2,1)S(1)} %bitcast.8, bf16[3,3,3,256,128]{4,3,2,1,0:T(8,128)(2,1)S(1)} %copy-done, f32[1,128]{1,0:T(1,128)S(1)} %bitcast.10, ...), custom_call_target="tpu_custom_call", output_to_operand_aliasing={{1}: (3, {})} | custom-call | flops 134217728 | bytes 1048576 | tf_op jit(solution)/shard_map/pallas_call | solution.py:28
  (3 shorter events, 0.1 us)
Async XLA Ops:
  1.6 17.5 %collective-permute-start = (bf16[3,4,32,128]{3,2,1,0:T(8,128)(2,1)S(1)}, bf16[3,4,32,128]{3,2,1,0:T(8,128)(2,1)S(1)}, u32[]{:S(2)}, u32[]{:S(2)}) collective-permute-start(bf16[3,4,32,128]{3,2,1,0:T(8,128)(2,1)S(1)} %get-tuple-element.19), channel_id=1, source_target_pairs={{0,4},{4,0},{8,12},{12,8},{16,20},{20,16},{24,28},{28,24},{32,36},... | collective-permute-start | bytes 294920 | tf_op jit(solution)/shard_map/ppermute | solution.py:20
  4.7 15.0 %collective-permute-start.1 = (bf16[3,4,32,128]{3,2,1,0:T(8,128)(2,1)S(1)}, bf16[3,4,32,128]{3,2,1,0:T(8,128)(2,1)S(1)}, u32[]{:S(2)}, u32[]{:S(2)}) collective-permute-start(bf16[3,4,32,128]{3,2,1,0:T(8,128)(2,1)S(1)} %get-tuple-element.20), channel_id=1, source_target_pairs={{4,8},{12,16},{20,24},{28,32},{36,40},{44,48},{52,56},{60,64},{68,... | collective-permute-start | bytes 294920 | tf_op jit(solution)/shard_map/ppermute | solution.py:19
  23.2 14.5 %copy-start.2 = (bf16[3,3,3,128,64]{3,4,2,1,0:T(8,128)(2,1)S(1)}, bf16[3,3,3,128,64]{3,4,2,1,0:T(8,128)(2,1)}, u32[]{:S(2)}) copy-start(bf16[3,3,3,128,64]{3,4,2,1,0:T(8,128)(2,1)} %param.10) | copy-start | bytes 1327108
  23.2 14.5 %copy-start.3 = (f32[64]{0:T(128)S(1)}, f32[64]{0:T(128)}, u32[]{:S(2)}) copy-start(f32[64]{0:T(128)} %param.11) | copy-start | bytes 772
  25.2 36.2 %copy-start = (bf16[3,3,3,256,128]{4,3,2,1,0:T(8,128)(2,1)S(1)}, bf16[3,3,3,256,128]{4,3,2,1,0:T(8,128)(2,1)}, u32[]{:S(2)}) copy-start(bf16[3,3,3,256,128]{4,3,2,1,0:T(8,128)(2,1)} %kernel.3) | copy-start | bytes 5308420
  25.2 36.2 %copy-start.1 = (f32[128]{0:T(128)S(1)}, f32[128]{0:T(128)}, u32[]{:S(2)}) copy-start(f32[128]{0:T(128)} %param.13) | copy-start | bytes 1540
  39.5 10.7 %collective-permute-start.2 = (bf16[1,4,8,64]{3,2,1,0:T(8,128)(2,1)S(1)}, bf16[1,4,8,64]{3,2,1,0:T(8,128)(2,1)S(1)}, u32[]{:S(2)}, u32[]{:S(2)}) collective-permute-start(bf16[1,4,8,64]{3,2,1,0:T(8,128)(2,1)S(1)} %get-tuple-element.26), channel_id=1, source_target_pairs={{0,4},{4,0},{8,12},{12,8},{16,20},{20,16},{24,28},{28,24},{32,36},... | collective-permute-start | bytes 12296 | tf_op jit(solution)/shard_map/ppermute | solution.py:20
  41.4 9.8 %collective-permute-start.3 = (bf16[1,4,8,64]{3,2,1,0:T(8,128)(2,1)S(1)}, bf16[1,4,8,64]{3,2,1,0:T(8,128)(2,1)S(1)}, u32[]{:S(2)}, u32[]{:S(2)}) collective-permute-start(bf16[1,4,8,64]{3,2,1,0:T(8,128)(2,1)S(1)} %get-tuple-element.26), channel_id=1, source_target_pairs={{4,8},{12,16},{20,24},{28,32},{36,40},{44,48},{52,56},{60,64},{68,... | collective-permute-start | bytes 12296 | tf_op jit(solution)/shard_map/ppermute | solution.py:19

commit v4 on v3

--- a/solution.py
+++ b/solution.py
@@ -12,13 +12,21 @@
     return [[i, i + 1] for i in range(0, peers, 2)]
 
 
-def swap(outward, inward, axis):
-    peers = lax.axis_size(axis)
-    even = [(i, i ^ 1) for i in range(peers)]
-    odd = [(i, i + 1) for i in range(1, peers - 1, 2)]
-    across = lax.ppermute(outward, axis, odd + [(j, i) for i, j in odd])
-    pair = lax.ppermute(inward, axis, even)
+def odd_groups(peers, cores):
+    inner = [[i * cores + c, (i + 1) * cores + c] for i in range(1, peers - 1, 2) for c in range(cores)]
+    return inner + [[i * cores + c, i * cores + c + 1] for i in (0, peers - 1) for c in range(0, cores, 2)]
+
+
+def swap(outward, inward):
+    peers, cores = lax.axis_size("gz"), lax.axis_size("gy")
+    pair = lax.ppermute(inward, "gz", [(i, i ^ 1) for i in range(peers)])
+    across = lax.all_gather(outward, ("gz", "gy"), axis_index_groups=odd_groups(peers, cores))
     return pair, across
+
+
+def at_end():
+    gz = lax.axis_index("gz")
+    return (gz == 0) | (gz == lax.axis_size("gz") - 1)
 
 
 def local(body, inputs, outs, scratch=(), flops=0, kept=(), sems=0, same={}):
@@ -48,37 +56,41 @@
 TAPS = [(i, j) for i in range(3) for j in range(3)]
 
 
-def edges(volume, own, outward, inward, sem):
+def edges(volume, kernel, bias, own, outward, inward, weights, offset, sem):
     odd = lax.axis_index("gz") % 2
     read = pltpu.make_async_copy(volume, own, sem.at[0])
     read.start()
+    others = [pltpu.make_async_copy(kernel.at[i], weights.at[i], sem.at[i + 1]) for i in range(3)]
+    others.append(pltpu.make_async_copy(bias, offset, sem.at[4]))
+    for other in others:
+        other.start()
     read.wait()
     outward[...] = own[pl.ds(odd, 3)]
     inward[...] = own[pl.ds(1 - odd, 3)]
-
-
-def fetch(kernel, bias, weights, offset, sem):
-    reads = [pltpu.make_async_copy(bias, offset, sem.at[27])]
-    for n, (i, j) in enumerate(TAPS):
-        for tap in range(3):
-            block = weights.at[128 * n : 128 * n + 128, 128 * tap : 128 * tap + 128]
-            reads.append(pltpu.make_async_copy(kernel.at[i, j, tap], block, sem.at[3 * n + tap]))
-    for read in reads:
-        read.start()
-    for read in reads:
-        read.wait()
+    for other in others:
+        other.wait()
+
+
+def stacked(kernel, axis):
+    taps = [jnp.concatenate([kernel[i, j, tap] for tap in range(3)], axis=axis) for i, j in TAPS]
+    return jnp.concatenate(taps, axis=1 - axis)
 
 
 def join(volume, pair, across, wide, rows):
     odd, gy = lax.axis_index("gz") % 2, lax.axis_index("gy")
     wide[3:7] = volume[...]
     wide[pl.ds(7 * (1 - odd), 3)] = pair[...]
-    wide[pl.ds(7 * odd, 3)] = across[...]
+    wide[pl.ds(7 * odd, 3)] = across[odd]
+
+    @pl.when(at_end())
+    def _():
+        wide[pl.ds(7 * odd, 3)] = jnp.zeros((3, 4, 32, 128), BF16)
+
     rows[0] = wide[:, 3 * (1 - gy % 2)]
     rows[1] = wide[:, jnp.where(gy < 2, 2, 1)]
 
 
-def level_a(wide, rows, weights, bias, skip, ship, x, most, own, sem):
+def level_a(wide, rows, kernel, bias, skip, ship, x, most):
     gy = lax.axis_index("gy")
     core = gy % 2
     x[:, 1:5] = wide[...]
@@ -86,16 +98,14 @@
     x[:, 5 * core] = jnp.zeros((10, 32, 128), BF16)
     open_row = jnp.where(gy == 1, 3, jnp.where(gy == 2, 0, 4))
     row = lax.broadcasted_iota(jnp.int32, (256, 128), 0) // 32 % 4
+    weights = stacked(kernel, 1)
     for p in (1, 2, 0, 3):
         z = 2 * p
         cells = jnp.concatenate([x[z + i : z + i + 2, j : j + 4].reshape(256, 128) for i, j in TAPS], axis=1)
-        sums = jnp.dot(cells, weights[...], preferred_element_type=F32)
+        sums = jnp.dot(cells, weights, preferred_element_type=F32)
         out = jnp.maximum(three_taps(sums, 32, 128) + bias[...], 0.0)
         if p in (1, 2):
-            own[z - 2 : z] = out.astype(BF16).reshape(2, 4, 32, 128)
-        if p == 2:
-            write = pltpu.make_async_copy(own, skip, sem.at[0])
-            write.start()
+            skip[z - 2 : z] = out.astype(BF16).reshape(2, 4, 32, 128)
         closed = jnp.where(row == open_row, 0.0, out)
         most[...] = jnp.max(closed.reshape(2, 2, 2, 32, 128), axis=(0, 2)).reshape(64, 128)
         small = jnp.maximum(most[pl.ds(0, 32, stride=2)], most[pl.ds(1, 32, stride=2)])
@@ -109,18 +119,19 @@
     def _():
         ship[4:14] = rows[1 - core, 1]
 
-    write.wait()
-
-
-def level_b(ships, weights_a, bias_a, kernel, bias, patch, skip, pooled, x, most_a, most):
+
+def level_b(ships, kernel_a, bias_a, kernel, bias, skip_a, patch, skip, pooled, out_a, x, most_a, most, sem):
     gz, gy = lax.axis_index("gz"), lax.axis_index("gy")
+    write = pltpu.make_async_copy(skip_a, out_a, sem.at[0])
+    write.start()
+    weights_a = stacked(kernel_a, 1)
     x[:, 0] = jnp.zeros((4, 16, 128), BF16)
     x[:, 9] = jnp.zeros((4, 16, 128), BF16)
     for g in range(4):
         x[:, 2 * g + 1 : 2 * g + 3] = ships[g, 0:4].reshape(4, 2, 16, 128)
     for r in range(2):
         cells = jnp.concatenate([ships[r + j, 4 + i : 12 + i].reshape(256, 128) for i, j in TAPS], axis=1)
-        sums = jnp.dot(cells, weights_a[...], preferred_element_type=F32)
+        sums = jnp.dot(cells, weights_a, preferred_element_type=F32)
         out = jnp.maximum(three_taps(sums, 32, 128) + bias_a[...], 0.0)
 
         @pl.when(gy == r + 1)
@@ -139,9 +150,7 @@
     def _():
         x[3] = jnp.zeros((10, 16, 128), BF16)
 
-    weights = jnp.concatenate(
-        [jnp.concatenate([kernel[i, j, tap] for tap in range(3)], axis=0) for i, j in TAPS], axis=1
-    )
+    weights = stacked(kernel, 0)
     cells = jnp.concatenate([x[i : i + 2, j : j + 8].reshape(256, 128) for i, j in TAPS], axis=1)
     sums = lax.dot_general(cells, weights, (((1,), (1,)), ((), ())), preferred_element_type=F32)
     out = jnp.maximum(three_taps(sums, 16, 64) + bias[...], 0.0)
@@ -149,6 +158,7 @@
     most[...] = jnp.max(out.reshape(2, 4, 2, 16, 64), axis=(0, 2)).reshape(64, 64)
     small = jnp.maximum(most[pl.ds(0, 32, stride=2)], most[pl.ds(1, 32, stride=2)])
     pooled[...] = small.astype(BF16).reshape(1, 4, 8, 64)
+    write.wait()
 
 
 def level_c(shards, kernel, bias, skip_a, patch, skip_b, bottom, out_a, out_b, x, sem):
@@ -165,9 +175,7 @@
     x[:, 0] = jnp.zeros((3, 8, 256), BF16)
     x[:, 5] = jnp.zeros((3, 8, 256), BF16)
     x[:, 1:5] = jnp.concatenate([shards[g] for g in range(4)], axis=-1)
-    weights = jnp.concatenate(
-        [jnp.concatenate([kernel[i, j, tap] for tap in range(3)], axis=1) for i, j in TAPS], axis=0
-    )
+    weights = stacked(kernel, 1)
     cells = jnp.concatenate([x[i, j : j + 4].reshape(32, 256) for i, j in TAPS], axis=1)
     sums = jnp.dot(cells, weights, preferred_element_type=F32)
     out = jnp.maximum(three_taps(sums, 8, 128) + bias[...], 0.0)
@@ -181,31 +189,35 @@
 
 def levels(volume, kernel_a, bias_a, kernel_b, bias_b, kernel_c, bias_c):
     slab = ((3, 4, 32, 128), BF16)
-    own, outward, inward = local(edges, (volume,), [((4, 4, 32, 128), BF16), slab, slab], kept=(0,), sems=1)
-    pair, across = swap(outward, inward, "gz")
-    weights, offset = local(
-        fetch, (kernel_a, bias_a[None]), [((1152, 384), BF16), ((1, 128), F32)], kept=(0, 1), sems=28
-    )
+    own, outward, inward, weights, offset = local(
+        edges,
+        (volume, kernel_a, bias_a[None]),
+        [((4, 4, 32, 128), BF16), slab, slab, (kernel_a.shape, BF16), ((1, 128), F32)],
+        kept=(0, 1, 2),
+        sems=5,
+    )
+    pair, across = swap(outward, inward)
     wide, rows = local(join, (own, pair, across), [((10, 4, 32, 128), BF16), ((2, 10, 32, 128), BF16)])
     rows = lax.all_gather(rows, "gy", axis_index_groups=even_groups(4))
     skip_a, ship = local(
         level_a,
         (wide, rows, weights, offset),
         [((4, 4, 32, 128), BF16), ((14, 32, 128), BF16)],
-        [((10, 6, 32, 128), BF16), ((64, 128), F32), ((4, 4, 32, 128), BF16)],
+        [((10, 6, 32, 128), BF16), ((64, 128), F32)],
         1 << 30,
-        kept=(4,),
-        sems=1,
-    )
-    patch, skip_b, pooled_b = local(
+    )
+    patch, skip_b, pooled_b, skip_a = local(
         level_b,
-        (lax.all_gather(ship, "gy"), weights, offset, jnp.swapaxes(kernel_b, 3, 4), bias_b[None]),
-        [((4, 32, 128), BF16), ((2, 8, 16, 64), BF16), ((1, 4, 8, 64), BF16)],
+        (lax.all_gather(ship, "gy"), weights, offset, jnp.swapaxes(kernel_b, 3, 4), bias_b[None], skip_a),
+        [((4, 32, 128), BF16), ((2, 8, 16, 64), BF16), ((1, 4, 8, 64), BF16), ((4, 4, 32, 128), BF16)],
         [((4, 10, 16, 128), BF16), ((128, 128), F32), ((64, 64), F32)],
         1 << 29,
-    )
-    pair, across = swap(pooled_b, pooled_b, "gz")
+        kept=(9,),
+        sems=1,
+    )
+    pair, across = swap(pooled_b, pooled_b)
     odd = lax.axis_index("gz") % 2
+    across = jnp.where(at_end(), BF16(0), lax.dynamic_index_in_dim(across, odd, 0, keepdims=False))
     deep = jnp.concatenate([jnp.where(odd == 1, pair, across), pooled_b, jnp.where(odd == 1, across, pair)])
     bottom, skip_a, skip_b = local(
         level_c,

time: 63.2 us -> 60.7 us (0.960)
  the two profiles are of different devices: /device:TPU:57 before, /device:TPU:8 now
where the time goes in v4:
time: 60.7 us; the launch traced here: 59.9 us
  blocking collectives  47.7 us (79%)
  Pallas kernels  6.12 us (10%)
  starting transfers between devices  5.32 us (9%)
  between operations  0.73 us (1%)
    all_gather x2, blocking collectives, swap(): lax.all_gather(outward, ('gz', 'gy'), axis_index_groups=odd_groups(peers,...  22.3 us
    all_gather x1, blocking collectives, levels(): lax.all_gather(ship, 'gy')  13.8 us
    all_gather x1, blocking collectives, levels(): lax.all_gather(deep, 'gy')  9.59 us
    pallas_call x5, Pallas kernels, local(): pl.pallas_call(body, out_shape=[jax.ShapeDtypeStruct(*out) for out in out...  6.12 us
    ppermute x2, starting transfers between devices, swap(): pair = lax.ppermute(inward, 'gz', [(i, i ^ 1) for i in range(peers)])  5.32 us
    all_gather x1, blocking collectives, levels(): rows = lax.all_gather(rows, 'gy', axis_index_groups=even_groups(4))  2.04 us
  transfers between devices with their start and end apart: 2, of which 0 were waited for; matrix products, arithmetic and copies ran while one was open for 0% of the time, Pallas kernels for 0%

profile of v4, /device:TPU:8, one launch (start us, length us, event | category | flops | bytes accessed | tf_op | source)
XLA Modules:
  0.0 59.9 jit_solution(2014206506849339923)
XLA Ops:
  0.6 1.3 %shard_map.94 = (bf16[4,4,32,128]{3,2,1,0:T(8,128)(2,1)S(1)}, bf16[3,4,32,128]{3,2,1,0:T(8,128)(2,1)S(1)}, bf16[3,4,32,128]{3,2,1,0:T(8,128)(2,1)S(1)}, bf16[3,3...) custom-call(bf16[4,4,32,128]{3,2,1,0:T(8,128)(2,1)} %volume.1, bf16[3,3,3,128,128]{4,3,2,1,0:T(8,128)(2,1)} %kernel.2, ...), custom_call_target="tpu_custom_call" | custom-call | bytes 1048576 | tf_op jit(solution)/shard_map/pallas_call | solution.py:36
  1.9 3.4 %collective-permute-start = (bf16[3,4,32,128]{3,2,1,0:T(8,128)(2,1)S(1)}, bf16[3,4,32,128]{3,2,1,0:T(8,128)(2,1)S(1)}, u32[]{:S(2)}, u32[]{:S(2)}) collective-permute-start(bf16[3,4,32,128]{3,2,1,0:T(8,128)(2,1)S(1)} %get-tuple-element.20), channel_id=1, source_target_pairs={{0,4},{4,0},{8,12},{12,8},{16,20},{20,16},{24,28},{28,24},{32,36},... | collective-permute-start | bytes 294920 | tf_op jit(solution)/shard_map/ppermute | solution.py:22
  5.3 13.7 %all-gather = bf16[6,4,32,128]{3,2,1,0:T(8,128)(2,1)S(1)} all-gather(bf16[3,4,32,128]{3,2,1,0:T(8,128)(2,1)S(1)} %get-tuple-element.21), channel_id=2, replica_groups={{4,8},{5,9},{6,10},{7,11},{12,16},{13,17},{14,18},{15,19},{20,24},{21,2..., dimensions={0}, use_global_device_ids=true | all-gather | bytes 294912 | tf_op jit(solution)/shard_map/all_gather | solution.py:23
  19.0 0.0 collective-permute-done.pair
  19.1 2.0 %all-gather.1 = bf16[4,10,32,128]{3,2,1,0:T(8,128)(2,1)S(1)} all-gather(bf16[2,10,32,128]{3,2,1,0:T(8,128)(2,1)S(1)} %get-tuple-element.23), channel_id=3, replica_groups={{0,1},{2,3},{4,5},{6,7},{8,9},{10,11},{12,13},{14,15},{16,17},{18,19},{..., dimensions={0}, use_global_device_ids=true | all-gather | bytes 491520 | tf_op jit(solution)/shard_map/all_gather | solution.py:201
  21.1 0.0 copy-start.2
  21.1 0.0 copy-start.3
  21.1 1.5 %shard_map.96 = (bf16[4,4,32,128]{3,2,1,0:T(8,128)(2,1)S(1)}, bf16[14,32,128]{2,1,0:T(8,128)(2,1)S(1)}) custom-call(bf16[10,4,32,128]{3,2,1,0:T(8,128)(2,1)S(1)} %get-tuple-element.22.wide, bf16[2,2,10,32,128]{4,3,2,1,0:T(8,128)(2,1)S(1)} %bitcast.11, bf16[3,3,3,128,128]{4,3,2,1,0:T(8,128)(2,1)S(1)} %get-tuple-element.24.kernel.kernel_a, ...), custom_call_target="tpu_custom_call" | custom-call | flops 1073741824 | bytes 1048576 | tf_op jit(solution)/shard_map/pallas_call | solution.py:36
  22.6 0.0 copy-start
  22.7 0.0 copy-start.1
  22.7 13.8 %all-gather.2 = bf16[56,32,128]{2,1,0:T(8,128)(2,1)S(1)} all-gather(bf16[14,32,128]{2,1,0:T(8,128)(2,1)S(1)} %get-tuple-element.26), channel_id=4, replica_groups=mesh['gz'=128,'gy'=4] {'gy'}, dimensions={0}, use_global_device_ids=true | all-gather | bytes 573440 | tf_op jit(solution)/shard_map/all_gather | solution.py:211
  36.5 0.0 copy-done.2
  36.5 0.0 copy-done.3
  36.5 1.8 %shard_map.97 = (bf16[4,32,128]{2,1,0:T(8,128)(2,1)S(1)}, bf16[2,8,16,64]{3,2,1,0:T(8,128)(2,1)S(1)}, bf16[1,4,8,64]{3,2,1,0:T(8,128)(2,1)S(1)}, bf16[4,4,32,128]{3,2,1,0:T(8,128)(2,1)}) custom-call(bf16[4,14,32,128]{3,2,1,0:T(8,128)(2,1)S(1)} %bitcast.9, bf16[3,3,3,128,128]{4,3,2,1,0:T(8,128)(2,1)S(1)} %get-tuple-element.24.kernel.kernel_a, ...), custom_call_target="tpu_custom_call" | custom-call | flops 536870912 | bytes 1048576 | tf_op jit(solution)/shard_map/pallas_call | solution.py:36
  38.3 1.9 %collective-permute-start.1 = (bf16[1,4,8,64]{3,2,1,0:T(8,128)(2,1)S(1)}, bf16[1,4,8,64]{3,2,1,0:T(8,128)(2,1)S(1)}, u32[]{:S(2)}, u32[]{:S(2)}) collective-permute-start(bf16[1,4,8,64]{3,2,1,0:T(8,128)(2,1)S(1)} %get-tuple-element.28), channel_id=1, source_target_pairs={{0,4},{4,0},{8,12},{12,8},{16,20},{20,16},{24,28},{28,24},{32,36},... | collective-permute-start | bytes 12296 | tf_op jit(solution)/shard_map/ppermute | solution.py:22
  40.2 8.6 %all-gather.3 = bf16[2,4,8,64]{3,2,1,0:T(8,128)(2,1)S(1)} all-gather(bf16[1,4,8,64]{3,2,1,0:T(8,128)(2,1)S(1)} %get-tuple-element.28), channel_id=5, replica_groups={{4,8},{5,9},{6,10},{7,11},{12,16},{13,17},{14,18},{15,19},{20,24},{21,2..., dimensions={0}, use_global_device_ids=true | all-gather | bytes 12288 | tf_op jit(solution)/shard_map/all_gather | solution.py:23
  48.8 0.0 collective-permute-done.1
  48.8 9.6 %all-gather.4 = bf16[12,4,8,64]{3,2,1,0:T(8,128)(2,1)S(1)} all-gather(bf16[3,4,8,64]{3,2,1,0:T(8,128)(2,1)S(1)} %pad_maximum_fusion), channel_id=6, replica_groups=mesh['gz'=128,'gy'=4] {'gy'}, dimensions={0}, use_global_device_ids=true | all-gather | bytes 61440 | tf_op jit(solution)/shard_map/all_gather | solution.py:224
  58.4 0.0 copy-done
  58.4 0.0 copy-done.1
  58.4 1.5 %shard_map.98 = (bf16[1,4,8,128]{3,2,1,0:T(8,128)(2,1)}, bf16[4,4,32,128]{3,2,1,0:T(8,128)(2,1)}, bf16[2,8,16,64]{3,2,1,0:T(8,128)(2,1)}) custom-call(bf16[4,3,4,8,64]{4,3,2,1,0:T(8,128)(2,1)S(1)} %bitcast.10, bf16[3,3,3,256,128]{4,3,2,1,0:T(8,128)(2,1)S(1)} %copy-done, f32[1,128]{1,0:T(1,128)S(1)} %bitcast.12, ...), custom_call_target="tpu_custom_call", output_to_operand_aliasing={{1}: (3, {})} | custom-call | flops 134217728 | bytes 1048576 | tf_op jit(solution)/shard_map/pallas_call | solution.py:36
  (3 shorter events, 0.1 us)
Async XLA Ops:
  1.9 17.1 %collective-permute-start = (bf16[3,4,32,128]{3,2,1,0:T(8,128)(2,1)S(1)}, bf16[3,4,32,128]{3,2,1,0:T(8,128)(2,1)S(1)}, u32[]{:S(2)}, u32[]{:S(2)}) collective-permute-start(bf16[3,4,32,128]{3,2,1,0:T(8,128)(2,1)S(1)} %get-tuple-element.20), channel_id=1, source_target_pairs={{0,4},{4,0},{8,12},{12,8},{16,20},{20,16},{24,28},{28,24},{32,36},... | collective-permute-start | bytes 294920 | tf_op jit(solution)/shard_map/ppermute | solution.py:22
  21.1 15.4 %copy-start.2 = (bf16[3,3,3,128,64]{3,4,2,1,0:T(8,128)(2,1)S(1)}, bf16[3,3,3,128,64]{3,4,2,1,0:T(8,128)(2,1)}, u32[]{:S(2)}) copy-start(bf16[3,3,3,128,64]{3,4,2,1,0:T(8,128)(2,1)} %param.10) | copy-start | bytes 1327108
  21.1 15.4 %copy-start.3 = (f32[64]{0:T(128)S(1)}, f32[64]{0:T(128)}, u32[]{:S(2)}) copy-start(f32[64]{0:T(128)} %param.11) | copy-start | bytes 772
  22.6 35.8 %copy-start = (bf16[3,3,3,256,128]{4,3,2,1,0:T(8,128)(2,1)S(1)}, bf16[3,3,3,256,128]{4,3,2,1,0:T(8,128)(2,1)}, u32[]{:S(2)}) copy-start(bf16[3,3,3,256,128]{4,3,2,1,0:T(8,128)(2,1)} %kernel.3) | copy-start | bytes 5308420
  22.7 35.8 %copy-start.1 = (f32[128]{0:T(128)S(1)}, f32[128]{0:T(128)}, u32[]{:S(2)}) copy-start(f32[128]{0:T(128)} %param.13) | copy-start | bytes 1540
  38.3 10.5 %collective-permute-start.1 = (bf16[1,4,8,64]{3,2,1,0:T(8,128)(2,1)S(1)}, bf16[1,4,8,64]{3,2,1,0:T(8,128)(2,1)S(1)}, u32[]{:S(2)}, u32[]{:S(2)}) collective-permute-start(bf16[1,4,8,64]{3,2,1,0:T(8,128)(2,1)S(1)} %get-tuple-element.28), channel_id=1, source_target_pairs={{0,4},{4,0},{8,12},{12,8},{16,20},{20,16},{24,28},{28,24},{32,36},... | collective-permute-start | bytes 12296 | tf_op jit(solution)/shard_map/ppermute | solution.py:22

commit v5 on v4

--- a/solution.py
+++ b/solution.py
@@ -12,21 +12,12 @@
     return [[i, i + 1] for i in range(0, peers, 2)]
 
 
-def odd_groups(peers, cores):
-    inner = [[i * cores + c, (i + 1) * cores + c] for i in range(1, peers - 1, 2) for c in range(cores)]
-    return inner + [[i * cores + c, i * cores + c + 1] for i in (0, peers - 1) for c in range(0, cores, 2)]
-
-
 def swap(outward, inward):
-    peers, cores = lax.axis_size("gz"), lax.axis_size("gy")
+    peers = lax.axis_size("gz")
+    odd = [(i, i + 1) for i in range(1, peers - 1, 2)]
     pair = lax.ppermute(inward, "gz", [(i, i ^ 1) for i in range(peers)])
-    across = lax.all_gather(outward, ("gz", "gy"), axis_index_groups=odd_groups(peers, cores))
+    across = lax.ppermute(outward, "gz", odd + [(j, i) for i, j in odd])
     return pair, across
-
-
-def at_end():
-    gz = lax.axis_index("gz")
-    return (gz == 0) | (gz == lax.axis_size("gz") - 1)
 
 
 def local(body, inputs, outs, scratch=(), flops=0, kept=(), sems=0, same={}):
@@ -80,12 +71,7 @@
     odd, gy = lax.axis_index("gz") % 2, lax.axis_index("gy")
     wide[3:7] = volume[...]
     wide[pl.ds(7 * (1 - odd), 3)] = pair[...]
-    wide[pl.ds(7 * odd, 3)] = across[odd]
-
-    @pl.when(at_end())
-    def _():
-        wide[pl.ds(7 * odd, 3)] = jnp.zeros((3, 4, 32, 128), BF16)
-
+    wide[pl.ds(7 * odd, 3)] = across[...]
     rows[0] = wide[:, 3 * (1 - gy % 2)]
     rows[1] = wide[:, jnp.where(gy < 2, 2, 1)]
 
@@ -217,7 +203,6 @@
     )
     pair, across = swap(pooled_b, pooled_b)
     odd = lax.axis_index("gz") % 2
-    across = jnp.where(at_end(), BF16(0), lax.dynamic_index_in_dim(across, odd, 0, keepdims=False))
     deep = jnp.concatenate([jnp.where(odd == 1, pair, across), pooled_b, jnp.where(odd == 1, across, pair)])
     bottom, skip_a, skip_b = local(
         level_c,

time: 60.7 us -> 63.1 us (1.040)
  blocking collectives: 47.7 us -> 25.4 us
  starting transfers between devices: 5.32 us -> 23.4 us
  waiting for transfers between devices: 0.01 us -> 6.57 us
    all_gather x2 -> x0, blocking collectives: 22.3 us -> none  [swap(): lax.all_gather(outward, ('gz', 'gy'), axis_index_groups=odd_groups(peers,...]
    ppermute x0 -> x2, starting transfers between devices: none -> 18.1 us  [swap(): across = lax.ppermute(outward, 'gz', odd + [(j, i) for i, j in odd])]
    ppermute x0 -> x2, waiting for transfers between devices: none -> 6.57 us  [swap(): across = lax.ppermute(outward, 'gz', odd + [(j, i) for i, j in odd])]
  transfers between devices with their start and end apart: 2 -> 4, of which waited for: 0 -> 2; matrix products, arithmetic and copies ran while one was open for 0% -> 0% of each run, Pallas kernels for 0% -> 0%
where the time goes in v5:
time: 63.1 us; the launch traced here: 62.3 us
  blocking collectives  25.4 us (40%)
  starting transfers between devices  23.4 us (37%)
  waiting for transfers between devices  6.57 us (10%)
  Pallas kernels  6.12 us (10%)
  between operations  0.74 us (1%)
    ppermute x2, starting transfers between devices, swap(): across = lax.ppermute(outward, 'gz', odd + [(j, i) for i, j in odd])  18.1 us
    all_gather x1, blocking collectives, levels(): lax.all_gather(ship, 'gy')  13.8 us
    all_gather x1, blocking collectives, levels(): lax.all_gather(deep, 'gy')  9.59 us
    ppermute x2, waiting for transfers between devices, swap(): across = lax.ppermute(outward, 'gz', odd + [(j, i) for i, j in odd])  6.57 us
    pallas_call x5, Pallas kernels, local(): pl.pallas_call(body, out_shape=[jax.ShapeDtypeStruct(*out) for out in out...  6.12 us
    ppermute x2, starting transfers between devices, swap(): pair = lax.ppermute(inward, 'gz', [(i, i ^ 1) for i in range(peers)])  5.32 us
    all_gather x1, blocking collectives, levels(): rows = lax.all_gather(rows, 'gy', axis_index_groups=even_groups(4))  2.04 us
  transfers between devices with their start and end apart: 4, of which 2 were waited for; matrix products, arithmetic and copies ran while one was open for 0% of the time, Pallas kernels for 0%

profile of v5, /device:TPU:8, one launch (start us, length us, event | category | flops | bytes accessed | tf_op | source)
XLA Modules:
  0.0 62.3 jit_solution(5813410901432672958)
XLA Ops:
  0.6 1.3 %shard_map.94 = (bf16[4,4,32,128]{3,2,1,0:T(8,128)(2,1)S(1)}, bf16[3,4,32,128]{3,2,1,0:T(8,128)(2,1)S(1)}, bf16[3,4,32,128]{3,2,1,0:T(8,128)(2,1)S(1)}, bf16[3,3...) custom-call(bf16[4,4,32,128]{3,2,1,0:T(8,128)(2,1)} %volume.1, bf16[3,3,3,128,128]{4,3,2,1,0:T(8,128)(2,1)} %kernel.2, ...), custom_call_target="tpu_custom_call" | custom-call | bytes 1048576 | tf_op jit(solution)/shard_map/pallas_call | solution.py:27
  1.9 3.4 %collective-permute-start = (bf16[3,4,32,128]{3,2,1,0:T(8,128)(2,1)S(1)}, bf16[3,4,32,128]{3,2,1,0:T(8,128)(2,1)S(1)}, u32[]{:S(2)}, u32[]{:S(2)}) collective-permute-start(bf16[3,4,32,128]{3,2,1,0:T(8,128)(2,1)S(1)} %get-tuple-element.20), channel_id=1, source_target_pairs={{0,4},{4,0},{8,12},{12,8},{16,20},{20,16},{24,28},{28,24},{32,36},... | collective-permute-start | bytes 294920 | tf_op jit(solution)/shard_map/ppermute | solution.py:18
  5.3 12.4 %collective-permute-start.1 = (bf16[3,4,32,128]{3,2,1,0:T(8,128)(2,1)S(1)}, bf16[3,4,32,128]{3,2,1,0:T(8,128)(2,1)S(1)}, u32[]{:S(2)}, u32[]{:S(2)}) collective-permute-start(bf16[3,4,32,128]{3,2,1,0:T(8,128)(2,1)S(1)} %get-tuple-element.21), channel_id=1, source_target_pairs={{4,8},{12,16},{20,24},{28,32},{36,40},{44,48},{52,56},{60,64},{68,... | collective-permute-start | bytes 294920 | tf_op jit(solution)/shard_map/ppermute | solution.py:19
  17.7 0.0 collective-permute-done.pair
  17.7 2.6 %collective-permute-done.1.across = bf16[3,4,32,128]{3,2,1,0:T(8,128)(2,1)S(1)} collective-permute-done((bf16[3,4,32,128]{3,2,1,0:T(8,128)(2,1)S(1)}, bf16[3,4,32,128]{3,2,1,0:T(8,128)(2,1)S(1)}, u32[]{:S(2)}, u32[]{:S(2)}) %collective-permute-start.1) | collective-permute-done | bytes 98336 | tf_op jit(solution)/shard_map/ppermute | solution.py:19
  20.3 2.0 %all-gather = bf16[4,10,32,128]{3,2,1,0:T(8,128)(2,1)S(1)} all-gather(bf16[2,10,32,128]{3,2,1,0:T(8,128)(2,1)S(1)} %get-tuple-element.23), channel_id=2, replica_groups={{0,1},{2,3},{4,5},{6,7},{8,9},{10,11},{12,13},{14,15},{16,17},{18,19},{..., dimensions={0}, use_global_device_ids=true | all-gather | bytes 491520 | tf_op jit(solution)/shard_map/all_gather | solution.py:187
  22.3 0.0 copy-start.2
  22.3 0.0 copy-start.3
  22.3 1.5 %shard_map.96 = (bf16[4,4,32,128]{3,2,1,0:T(8,128)(2,1)S(1)}, bf16[14,32,128]{2,1,0:T(8,128)(2,1)S(1)}) custom-call(bf16[10,4,32,128]{3,2,1,0:T(8,128)(2,1)S(1)} %get-tuple-element.22.wide, bf16[2,2,10,32,128]{4,3,2,1,0:T(8,128)(2,1)S(1)} %bitcast.9, bf16[3,3,3,128,128]{4,3,2,1,0:T(8,128)(2,1)S(1)} %get-tuple-element.24.kernel.kernel_a, ...), custom_call_target="tpu_custom_call" | custom-call | flops 1073741824 | bytes 1048576 | tf_op jit(solution)/shard_map/pallas_call | solution.py:27
  23.9 0.0 copy-start
  23.9 0.0 copy-start.1
  23.9 13.8 %all-gather.1 = bf16[56,32,128]{2,1,0:T(8,128)(2,1)S(1)} all-gather(bf16[14,32,128]{2,1,0:T(8,128)(2,1)S(1)} %get-tuple-element.26), channel_id=3, replica_groups=mesh['gz'=128,'gy'=4] {'gy'}, dimensions={0}, use_global_device_ids=true | all-gather | bytes 573440 | tf_op jit(solution)/shard_map/all_gather | solution.py:197
  37.7 0.0 copy-done.2
  37.7 0.0 copy-done.3
  37.7 1.8 %shard_map.97 = (bf16[4,32,128]{2,1,0:T(8,128)(2,1)S(1)}, bf16[2,8,16,64]{3,2,1,0:T(8,128)(2,1)S(1)}, bf16[1,4,8,64]{3,2,1,0:T(8,128)(2,1)S(1)}, bf16[4,4,32,128]{3,2,1,0:T(8,128)(2,1)}) custom-call(bf16[4,14,32,128]{3,2,1,0:T(8,128)(2,1)S(1)} %bitcast.7, bf16[3,3,3,128,128]{4,3,2,1,0:T(8,128)(2,1)S(1)} %get-tuple-element.24.kernel.kernel_a, ...), custom_call_target="tpu_custom_call" | custom-call | flops 536870912 | bytes 1048576 | tf_op jit(solution)/shard_map/pallas_call | solution.py:27
  39.5 1.9 %collective-permute-start.2 = (bf16[1,4,8,64]{3,2,1,0:T(8,128)(2,1)S(1)}, bf16[1,4,8,64]{3,2,1,0:T(8,128)(2,1)S(1)}, u32[]{:S(2)}, u32[]{:S(2)}) collective-permute-start(bf16[1,4,8,64]{3,2,1,0:T(8,128)(2,1)S(1)} %get-tuple-element.28), channel_id=1, source_target_pairs={{0,4},{4,0},{8,12},{12,8},{16,20},{20,16},{24,28},{28,24},{32,36},... | collective-permute-start | bytes 12296 | tf_op jit(solution)/shard_map/ppermute | solution.py:18
  41.4 5.7 %collective-permute-start.3 = (bf16[1,4,8,64]{3,2,1,0:T(8,128)(2,1)S(1)}, bf16[1,4,8,64]{3,2,1,0:T(8,128)(2,1)S(1)}, u32[]{:S(2)}, u32[]{:S(2)}) collective-permute-start(bf16[1,4,8,64]{3,2,1,0:T(8,128)(2,1)S(1)} %get-tuple-element.28), channel_id=1, source_target_pairs={{4,8},{12,16},{20,24},{28,32},{36,40},{44,48},{52,56},{60,64},{68,... | collective-permute-start | bytes 12296 | tf_op jit(solution)/shard_map/ppermute | solution.py:19
  47.2 0.0 collective-permute-done.2
  47.2 4.0 %collective-permute-done.3 = bf16[1,4,8,64]{3,2,1,0:T(8,128)(2,1)S(1)} collective-permute-done((bf16[1,4,8,64]{3,2,1,0:T(8,128)(2,1)S(1)}, bf16[1,4,8,64]{3,2,1,0:T(8,128)(2,1)S(1)}, u32[]{:S(2)}, u32[]{:S(2)}) %collective-permute-start.3) | collective-permute-done | bytes 4128 | tf_op jit(solution)/shard_map/ppermute | solution.py:19
  51.2 9.6 %all-gather.2 = bf16[12,4,8,64]{3,2,1,0:T(8,128)(2,1)S(1)} all-gather(bf16[3,4,8,64]{3,2,1,0:T(8,128)(2,1)S(1)} %pad_maximum_fusion), channel_id=4, replica_groups=mesh['gz'=128,'gy'=4] {'gy'}, dimensions={0}, use_global_device_ids=true | all-gather | bytes 61440 | tf_op jit(solution)/shard_map/all_gather | solution.py:209
  60.8 0.0 copy-done
  60.8 0.0 copy-done.1
  60.8 1.5 %shard_map.98 = (bf16[1,4,8,128]{3,2,1,0:T(8,128)(2,1)}, bf16[4,4,32,128]{3,2,1,0:T(8,128)(2,1)}, bf16[2,8,16,64]{3,2,1,0:T(8,128)(2,1)}) custom-call(bf16[4,3,4,8,64]{4,3,2,1,0:T(8,128)(2,1)S(1)} %bitcast.8, bf16[3,3,3,256,128]{4,3,2,1,0:T(8,128)(2,1)S(1)} %copy-done, f32[1,128]{1,0:T(1,128)S(1)} %bitcast.10, ...), custom_call_target="tpu_custom_call", output_to_operand_aliasing={{1}: (3, {})} | custom-call | flops 134217728 | bytes 1048576 | tf_op jit(solution)/shard_map/pallas_call | solution.py:27
  (3 shorter events, 0.1 us)
Async XLA Ops:
  1.9 15.8 %collective-permute-start = (bf16[3,4,32,128]{3,2,1,0:T(8,128)(2,1)S(1)}, bf16[3,4,32,128]{3,2,1,0:T(8,128)(2,1)S(1)}, u32[]{:S(2)}, u32[]{:S(2)}) collective-permute-start(bf16[3,4,32,128]{3,2,1,0:T(8,128)(2,1)S(1)} %get-tuple-element.20), channel_id=1, source_target_pairs={{0,4},{4,0},{8,12},{12,8},{16,20},{20,16},{24,28},{28,24},{32,36},... | collective-permute-start | bytes 294920 | tf_op jit(solution)/shard_map/ppermute | solution.py:18
  5.3 15.0 %collective-permute-start.1 = (bf16[3,4,32,128]{3,2,1,0:T(8,128)(2,1)S(1)}, bf16[3,4,32,128]{3,2,1,0:T(8,128)(2,1)S(1)}, u32[]{:S(2)}, u32[]{:S(2)}) collective-permute-start(bf16[3,4,32,128]{3,2,1,0:T(8,128)(2,1)S(1)} %get-tuple-element.21), channel_id=1, source_target_pairs={{4,8},{12,16},{20,24},{28,32},{36,40},{44,48},{52,56},{60,64},{68,... | collective-permute-start | bytes 294920 | tf_op jit(solution)/shard_map/ppermute | solution.py:19
  22.3 15.4 %copy-start.2 = (bf16[3,3,3,128,64]{3,4,2,1,0:T(8,128)(2,1)S(1)}, bf16[3,3,3,128,64]{3,4,2,1,0:T(8,128)(2,1)}, u32[]{:S(2)}) copy-start(bf16[3,3,3,128,64]{3,4,2,1,0:T(8,128)(2,1)} %param.10) | copy-start | bytes 1327108
  22.3 15.4 %copy-start.3 = (f32[64]{0:T(128)S(1)}, f32[64]{0:T(128)}, u32[]{:S(2)}) copy-start(f32[64]{0:T(128)} %param.11) | copy-start | bytes 772
  23.9 36.9 %copy-start = (bf16[3,3,3,256,128]{4,3,2,1,0:T(8,128)(2,1)S(1)}, bf16[3,3,3,256,128]{4,3,2,1,0:T(8,128)(2,1)}, u32[]{:S(2)}) copy-start(bf16[3,3,3,256,128]{4,3,2,1,0:T(8,128)(2,1)} %kernel.3) | copy-start | bytes 5308420
  23.9 36.9 %copy-start.1 = (f32[128]{0:T(128)S(1)}, f32[128]{0:T(128)}, u32[]{:S(2)}) copy-start(f32[128]{0:T(128)} %param.13) | copy-start | bytes 1540
  39.5 7.7 %collective-permute-start.2 = (bf16[1,4,8,64]{3,2,1,0:T(8,128)(2,1)S(1)}, bf16[1,4,8,64]{3,2,1,0:T(8,128)(2,1)S(1)}, u32[]{:S(2)}, u32[]{:S(2)}) collective-permute-start(bf16[1,4,8,64]{3,2,1,0:T(8,128)(2,1)S(1)} %get-tuple-element.28), channel_id=1, source_target_pairs={{0,4},{4,0},{8,12},{12,8},{16,20},{20,16},{24,28},{28,24},{32,36},... | collective-permute-start | bytes 12296 | tf_op jit(solution)/shard_map/ppermute | solution.py:18
  41.4 9.8 %collective-permute-start.3 = (bf16[1,4,8,64]{3,2,1,0:T(8,128)(2,1)S(1)}, bf16[1,4,8,64]{3,2,1,0:T(8,128)(2,1)S(1)}, u32[]{:S(2)}, u32[]{:S(2)}) collective-permute-start(bf16[1,4,8,64]{3,2,1,0:T(8,128)(2,1)S(1)} %get-tuple-element.28), channel_id=1, source_target_pairs={{4,8},{12,16},{20,24},{28,32},{36,40},{44,48},{52,56},{60,64},{68,... | collective-permute-start | bytes 12296 | tf_op jit(solution)/shard_map/ppermute | solution.py:19

commit v6 on v4

--- a/solution.py
+++ b/solution.py
@@ -56,19 +56,13 @@
 TAPS = [(i, j) for i in range(3) for j in range(3)]
 
 
-def edges(volume, kernel, bias, own, outward, inward, weights, offset, sem):
+def edges(volume, own, outward, inward, sem):
     odd = lax.axis_index("gz") % 2
     read = pltpu.make_async_copy(volume, own, sem.at[0])
     read.start()
-    others = [pltpu.make_async_copy(kernel.at[i], weights.at[i], sem.at[i + 1]) for i in range(3)]
-    others.append(pltpu.make_async_copy(bias, offset, sem.at[4]))
-    for other in others:
-        other.start()
     read.wait()
     outward[...] = own[pl.ds(odd, 3)]
     inward[...] = own[pl.ds(1 - odd, 3)]
-    for other in others:
-        other.wait()
 
 
 def stacked(kernel, axis):
@@ -161,7 +155,7 @@
     write.wait()
 
 
-def level_c(shards, kernel, bias, skip_a, patch, skip_b, bottom, out_a, out_b, x, sem):
+def level_c(own, pair, across, kernel, bias, skip_a, patch, skip_b, bottom, out_a, out_b, x, sem):
     gy = lax.axis_index("gy")
     write_b = pltpu.make_async_copy(skip_b, out_b, sem.at[0])
     write_b.start()
@@ -174,7 +168,15 @@
 
     x[:, 0] = jnp.zeros((3, 8, 256), BF16)
     x[:, 5] = jnp.zeros((3, 8, 256), BF16)
-    x[:, 1:5] = jnp.concatenate([shards[g] for g in range(4)], axis=-1)
+    odd = lax.axis_index("gz") % 2
+    x[1, 1:5] = jnp.concatenate([own[g] for g in range(4)], axis=-1)
+    x[2 * (1 - odd), 1:5] = jnp.concatenate([pair[g] for g in range(4)], axis=-1)
+    x[2 * odd, 1:5] = jnp.concatenate([across[odd, g] for g in range(4)], axis=-1)
+
+    @pl.when(at_end())
+    def _():
+        x[2 * odd, 1:5] = jnp.zeros((4, 8, 256), BF16)
+
     weights = stacked(kernel, 1)
     cells = jnp.concatenate([x[i, j : j + 4].reshape(32, 256) for i, j in TAPS], axis=1)
     sums = jnp.dot(cells, weights, preferred_element_type=F32)
@@ -189,45 +191,38 @@
 
 def levels(volume, kernel_a, bias_a, kernel_b, bias_b, kernel_c, bias_c):
     slab = ((3, 4, 32, 128), BF16)
-    own, outward, inward, weights, offset = local(
-        edges,
-        (volume, kernel_a, bias_a[None]),
-        [((4, 4, 32, 128), BF16), slab, slab, (kernel_a.shape, BF16), ((1, 128), F32)],
-        kept=(0, 1, 2),
-        sems=5,
-    )
+    own, outward, inward = local(edges, (volume,), [((4, 4, 32, 128), BF16), slab, slab], kept=(0,), sems=1)
     pair, across = swap(outward, inward)
-    wide, rows = local(join, (own, pair, across), [((10, 4, 32, 128), BF16), ((2, 10, 32, 128), BF16)])
+    joined = [((10, 4, 32, 128), BF16), ((2, 10, 32, 128), BF16)]
+    wide, rows = local(join, (own, pair, across), joined, flops=1 << 33)
     rows = lax.all_gather(rows, "gy", axis_index_groups=even_groups(4))
     skip_a, ship = local(
         level_a,
-        (wide, rows, weights, offset),
+        (wide, rows, kernel_a, bias_a[None]),
         [((4, 4, 32, 128), BF16), ((14, 32, 128), BF16)],
         [((10, 6, 32, 128), BF16), ((64, 128), F32)],
         1 << 30,
     )
     patch, skip_b, pooled_b, skip_a = local(
         level_b,
-        (lax.all_gather(ship, "gy"), weights, offset, jnp.swapaxes(kernel_b, 3, 4), bias_b[None], skip_a),
+        (lax.all_gather(ship, "gy"), kernel_a, bias_a[None], jnp.swapaxes(kernel_b, 3, 4), bias_b[None], skip_a),
         [((4, 32, 128), BF16), ((2, 8, 16, 64), BF16), ((1, 4, 8, 64), BF16), ((4, 4, 32, 128), BF16)],
         [((4, 10, 16, 128), BF16), ((128, 128), F32), ((64, 64), F32)],
         1 << 29,
         kept=(9,),
         sems=1,
     )
-    pair, across = swap(pooled_b, pooled_b)
-    odd = lax.axis_index("gz") % 2
-    across = jnp.where(at_end(), BF16(0), lax.dynamic_index_in_dim(across, odd, 0, keepdims=False))
-    deep = jnp.concatenate([jnp.where(odd == 1, pair, across), pooled_b, jnp.where(odd == 1, across, pair)])
+    channels = lax.all_gather(pooled_b, "gy", tiled=True)
+    pair, across = swap(channels, channels)
     bottom, skip_a, skip_b = local(
         level_c,
-        (lax.all_gather(deep, "gy"), kernel_c, bias_c[None], skip_a, patch, skip_b),
+        (channels, pair, across, kernel_c, bias_c[None], skip_a, patch, skip_b),
         [((1, 4, 8, 128), BF16), ((4, 4, 32, 128), BF16), ((2, 8, 16, 64), BF16)],
         [((3, 6, 8, 256), BF16)],
         1 << 27,
-        kept=(3, 7, 8),
+        kept=(5, 9, 10),
         sems=2,
-        same={3: 1},
+        same={5: 1},
     )
     return (skip_a, skip_b, bottom)
 

time: 60.7 us -> 59.7 us (0.984)
  the two profiles are of different devices: /device:TPU:8 before, /device:TPU:40 now
where the time goes in v6:
time: 59.7 us; the launch traced here: 59.5 us
  blocking collectives  47.9 us (80%)
  Pallas kernels  5.56 us (9%)
  starting transfers between devices  5.31 us (9%)
  between operations  0.71 us (1%)
    all_gather x2, blocking collectives, swap(): lax.all_gather(outward, ('gz', 'gy'), axis_index_groups=odd_groups(peers,...  23.4 us
    all_gather x1, blocking collectives, levels(): lax.all_gather(ship, 'gy')  13.2 us
    all_gather x1, blocking collectives, levels(): channels = lax.all_gather(pooled_b, 'gy', tiled=True)  9.1 us
    pallas_call x5, Pallas kernels, local(): pl.pallas_call(body, out_shape=[jax.ShapeDtypeStruct(*out) for out in out...  5.56 us
    ppermute x2, starting transfers between devices, swap(): pair = lax.ppermute(inward, 'gz', [(i, i ^ 1) for i in range(peers)])  5.31 us
    all_gather x1, blocking collectives, levels(): rows = lax.all_gather(rows, 'gy', axis_index_groups=even_groups(4))  2.17 us
  transfers between devices with their start and end apart: 2, of which 0 were waited for; matrix products, arithmetic and copies ran while one was open for 0% of the time, Pallas kernels for 0%

profile of v6, /device:TPU:40, one launch (start us, length us, event | category | flops | bytes accessed | tf_op | source)
XLA Modules:
  0.0 59.5 jit_solution(4439741077517700196)
XLA Ops:
  0.6 0.9 %shard_map.94 = (bf16[4,4,32,128]{3,2,1,0:T(8,128)(2,1)S(1)}, bf16[3,4,32,128]{3,2,1,0:T(8,128)(2,1)S(1)}, bf16[3,4,32,128]{3,2,1,0:T(8,128)(2,1)S(1)}) custom-call(bf16[4,4,32,128]{3,2,1,0:T(8,128)(2,1)} %volume.1), custom_call_target="tpu_custom_call" | custom-call | bytes 1048576 | tf_op jit(solution)/shard_map/pallas_call | solution.py:36
  1.6 3.4 %collective-permute-start = (bf16[3,4,32,128]{3,2,1,0:T(8,128)(2,1)S(1)}, bf16[3,4,32,128]{3,2,1,0:T(8,128)(2,1)S(1)}, u32[]{:S(2)}, u32[]{:S(2)}) collective-permute-start(bf16[3,4,32,128]{3,2,1,0:T(8,128)(2,1)S(1)} %get-tuple-element.18), channel_id=1, source_target_pairs={{0,4},{4,0},{8,12},{12,8},{16,20},{20,16},{24,28},{28,24},{32,36},... | collective-permute-start | bytes 294920 | tf_op jit(solution)/shard_map/ppermute | solution.py:22
  5.0 14.6 %all-gather = bf16[6,4,32,128]{3,2,1,0:T(8,128)(2,1)S(1)} all-gather(bf16[3,4,32,128]{3,2,1,0:T(8,128)(2,1)S(1)} %get-tuple-element.19), channel_id=2, replica_groups={{4,8},{5,9},{6,10},{7,11},{12,16},{13,17},{14,18},{15,19},{20,24},{21,2..., dimensions={0}, use_global_device_ids=true | all-gather | bytes 294912 | tf_op jit(solution)/shard_map/all_gather | solution.py:23
  19.6 0.0 collective-permute-done.pair
  19.6 0.0 copy-start.2
  19.6 0.0 copy-start.4
  19.6 2.2 %all-gather.1 = bf16[4,10,32,128]{3,2,1,0:T(8,128)(2,1)S(1)} all-gather(bf16[2,10,32,128]{3,2,1,0:T(8,128)(2,1)S(1)} %get-tuple-element.21), channel_id=3, replica_groups={{0,1},{2,3},{4,5},{6,7},{8,9},{10,11},{12,13},{14,15},{16,17},{18,19},{..., dimensions={0}, use_global_device_ids=true | all-gather | bytes 491520 | tf_op jit(solution)/shard_map/all_gather | solution.py:198
  21.8 0.0 copy-done.2
  21.8 0.0 copy-done.4
  21.8 0.0 copy-start.3
  21.8 0.0 copy-start.5
  21.8 1.5 %shard_map.96 = (bf16[4,4,32,128]{3,2,1,0:T(8,128)(2,1)S(1)}, bf16[14,32,128]{2,1,0:T(8,128)(2,1)S(1)}) custom-call(bf16[10,4,32,128]{3,2,1,0:T(8,128)(2,1)S(1)} %get-tuple-element.20.wide, bf16[2,2,10,32,128]{4,3,2,1,0:T(8,128)(2,1)S(1)} %bitcast.9, bf16[3,3,3,128,128]{4,3,2,1,0:T(8,128)(2,1)S(1)} %copy-done.2, f32[1,128]{1,0:T(1,128)S(1)} %bitcast.14), custom_call_target="tpu_custom_call" | custom-call | flops 1073741824 | bytes 1048576 | tf_op jit(solution)/shard_map/pallas_call | solution.py:36
  23.4 0.0 copy-start
  23.4 0.0 copy-start.1
  23.4 13.2 %all-gather.2 = bf16[56,32,128]{2,1,0:T(8,128)(2,1)S(1)} all-gather(bf16[14,32,128]{2,1,0:T(8,128)(2,1)S(1)} %get-tuple-element.22), channel_id=4, replica_groups=mesh['gz'=128,'gy'=4] {'gy'}, dimensions={0}, use_global_device_ids=true | all-gather | bytes 573440 | tf_op jit(solution)/shard_map/all_gather | solution.py:208
  36.6 0.0 copy-done.3
  36.6 0.0 copy-done.5
  36.6 1.8 %shard_map.97 = (bf16[4,32,128]{2,1,0:T(8,128)(2,1)S(1)}, bf16[2,8,16,64]{3,2,1,0:T(8,128)(2,1)S(1)}, bf16[1,4,8,64]{3,2,1,0:T(8,128)(2,1)S(1)}, bf16[4,4,32,128]{3,2,1,0:T(8,128)(2,1)}) custom-call(bf16[4,14,32,128]{3,2,1,0:T(8,128)(2,1)S(1)} %bitcast.8, bf16[3,3,3,128,128]{4,3,2,1,0:T(8,128)(2,1)S(1)} %copy-done.2, f32[1,128]{1,0:T(1,128)S(1)} %bitcast.15, ...), custom_call_target="tpu_custom_call" | custom-call | flops 536870912 | bytes 1048576 | tf_op jit(solution)/shard_map/pallas_call | solution.py:36
  38.4 9.1 %all_gather.33.own = bf16[4,4,8,64]{3,2,1,0:T(8,128)(2,1)S(1)} all-gather(bf16[1,4,8,64]{3,2,1,0:T(8,128)(2,1)S(1)} %get-tuple-element.24), channel_id=1, replica_groups=mesh['gz'=128,'gy'=4] {'gy'}, dimensions={0}, use_global_device_ids=true | all-gather | bytes 20480 | tf_op jit(solution)/shard_map/all_gather | solution.py:215
  47.5 1.9 %collective-permute-start.1 = (bf16[4,4,8,64]{3,2,1,0:T(8,128)(2,1)S(1)}, bf16[4,4,8,64]{3,2,1,0:T(8,128)(2,1)S(1)}, u32[]{:S(2)}, u32[]{:S(2)}) collective-permute-start(bf16[4,4,8,64]{3,2,1,0:T(8,128)(2,1)S(1)} %all_gather.33.own), channel_id=1, source_target_pairs={{0,4},{4,0},{8,12},{12,8},{16,20},{20,16},{24,28},{28,24},{32,36},... | collective-permute-start | bytes 49160 | tf_op jit(solution)/shard_map/ppermute | solution.py:22
  49.4 8.8 %all-gather.3 = bf16[8,4,8,64]{3,2,1,0:T(8,128)(2,1)S(1)} all-gather(bf16[4,4,8,64]{3,2,1,0:T(8,128)(2,1)S(1)} %all_gather.33.own), channel_id=5, replica_groups={{4,8},{5,9},{6,10},{7,11},{12,16},{13,17},{14,18},{15,19},{20,24},{21,2..., dimensions={0}, use_global_device_ids=true | all-gather | bytes 49152 | tf_op jit(solution)/shard_map/all_gather | solution.py:23
  58.2 0.0 collective-permute-done.1.pair
  58.2 0.0 copy-done
  58.2 0.0 copy-done.1
  58.2 1.3 %shard_map.98 = (bf16[1,4,8,128]{3,2,1,0:T(8,128)(2,1)}, bf16[4,4,32,128]{3,2,1,0:T(8,128)(2,1)}, bf16[2,8,16,64]{3,2,1,0:T(8,128)(2,1)}) custom-call(bf16[4,4,8,64]{3,2,1,0:T(8,128)(2,1)S(1)} %all_gather.33.own, bf16[4,4,8,64]{3,2,1,0:T(8,128)(2,1)S(1)} %collective-permute-done.1.pair, ...), custom_call_target="tpu_custom_call", output_to_operand_aliasing={{1}: (5, {})} | custom-call | flops 134217728 | bytes 1048576 | tf_op jit(solution)/shard_map/pallas_call | solution.py:36
  (1 shorter events, 0.0 us)
Async XLA Ops:
  1.6 18.0 %collective-permute-start = (bf16[3,4,32,128]{3,2,1,0:T(8,128)(2,1)S(1)}, bf16[3,4,32,128]{3,2,1,0:T(8,128)(2,1)S(1)}, u32[]{:S(2)}, u32[]{:S(2)}) collective-permute-start(bf16[3,4,32,128]{3,2,1,0:T(8,128)(2,1)S(1)} %get-tuple-element.18), channel_id=1, source_target_pairs={{0,4},{4,0},{8,12},{12,8},{16,20},{20,16},{24,28},{28,24},{32,36},... | collective-permute-start | bytes 294920 | tf_op jit(solution)/shard_map/ppermute | solution.py:22
  19.6 2.2 %copy-start.2 = (bf16[3,3,3,128,128]{4,3,2,1,0:T(8,128)(2,1)S(1)}, bf16[3,3,3,128,128]{4,3,2,1,0:T(8,128)(2,1)}, u32[]{:S(2)}) copy-start(bf16[3,3,3,128,128]{4,3,2,1,0:T(8,128)(2,1)} %kernel_a.1) | copy-start | bytes 2654212
  19.6 2.2 %copy-start.4 = (f32[128]{0:T(128)S(1)}, f32[128]{0:T(128)}, u32[]{:S(2)}) copy-start(f32[128]{0:T(128)} %param.9) | copy-start | bytes 1540
  21.8 14.8 %copy-start.3 = (bf16[3,3,3,128,64]{3,4,2,1,0:T(8,128)(2,1)S(1)}, bf16[3,3,3,128,64]{3,4,2,1,0:T(8,128)(2,1)}, u32[]{:S(2)}) copy-start(bf16[3,3,3,128,64]{3,4,2,1,0:T(8,128)(2,1)} %param.10) | copy-start | bytes 1327108
  21.8 14.8 %copy-start.5 = (f32[64]{0:T(128)S(1)}, f32[64]{0:T(128)}, u32[]{:S(2)}) copy-start(f32[64]{0:T(128)} %param.11) | copy-start | bytes 772
  23.4 34.9 %copy-start = (bf16[3,3,3,256,128]{4,3,2,1,0:T(8,128)(2,1)S(1)}, bf16[3,3,3,256,128]{4,3,2,1,0:T(8,128)(2,1)}, u32[]{:S(2)}) copy-start(bf16[3,3,3,256,128]{4,3,2,1,0:T(8,128)(2,1)} %kernel.3) | copy-start | bytes 5308420
  23.4 34.8 %copy-start.1 = (f32[128]{0:T(128)S(1)}, f32[128]{0:T(128)}, u32[]{:S(2)}) copy-start(f32[128]{0:T(128)} %param.13) | copy-start | bytes 1540
  47.5 10.7 %collective-permute-start.1 = (bf16[4,4,8,64]{3,2,1,0:T(8,128)(2,1)S(1)}, bf16[4,4,8,64]{3,2,1,0:T(8,128)(2,1)S(1)}, u32[]{:S(2)}, u32[]{:S(2)}) collective-permute-start(bf16[4,4,8,64]{3,2,1,0:T(8,128)(2,1)S(1)} %all_gather.33.own), channel_id=1, source_target_pairs={{0,4},{4,0},{8,12},{12,8},{16,20},{20,16},{24,28},{28,24},{32,36},... | collective-permute-start | bytes 49160 | tf_op jit(solution)/shard_map/ppermute | solution.py:22

commit v7 on v6

--- a/solution.py
+++ b/solution.py
@@ -82,6 +82,10 @@
 
     rows[0] = wide[:, 3 * (1 - gy % 2)]
     rows[1] = wide[:, jnp.where(gy < 2, 2, 1)]
+
+
+def masked(cells, inside):
+    return (cells.astype(F32) * jnp.where(inside, 1.0, 0.0)).astype(BF16)
 
 
 def level_a(wide, rows, kernel, bias, skip, ship, x, most):
@@ -115,7 +119,7 @@
 
 
 def level_b(ships, kernel_a, bias_a, kernel, bias, skip_a, patch, skip, pooled, out_a, x, most_a, most, sem):
-    gz, gy = lax.axis_index("gz"), lax.axis_index("gy")
+    gz = lax.axis_index("gz")
     write = pltpu.make_async_copy(skip_a, out_a, sem.at[0])
     write.start()
     weights_a = stacked(kernel_a, 1)
@@ -123,27 +127,19 @@
     x[:, 9] = jnp.zeros((4, 16, 128), BF16)
     for g in range(4):
         x[:, 2 * g + 1 : 2 * g + 3] = ships[g, 0:4].reshape(4, 2, 16, 128)
+    open_rows = []
     for r in range(2):
         cells = jnp.concatenate([ships[r + j, 4 + i : 12 + i].reshape(256, 128) for i, j in TAPS], axis=1)
         sums = jnp.dot(cells, weights_a, preferred_element_type=F32)
         out = jnp.maximum(three_taps(sums, 32, 128) + bias_a[...], 0.0)
-
-        @pl.when(gy == r + 1)
-        def _():
-            patch[...] = out[64:192].astype(BF16).reshape(4, 32, 128)
-
+        open_rows.append(out[64:192].astype(BF16).reshape(4, 32, 128))
         most_a[...] = jnp.max(out.reshape(4, 2, 32, 128), axis=1).reshape(128, 128)
         small = jnp.maximum(most_a[pl.ds(0, 64, stride=2)], most_a[pl.ds(1, 64, stride=2)])
         x[:, 4 + r] = jnp.maximum(x[:, 4 + r], small.astype(BF16).reshape(4, 16, 128))
-
-    @pl.when(gz == 0)
-    def _():
-        x[0] = jnp.zeros((10, 16, 128), BF16)
-
-    @pl.when(gz == lax.axis_size("gz") - 1)
-    def _():
-        x[3] = jnp.zeros((10, 16, 128), BF16)
-
+    patch[0] = open_rows[0]
+    patch[1] = open_rows[1]
+    x[0] = masked(x[0], gz > 0)
+    x[3] = masked(x[3], gz < lax.axis_size("gz") - 1)
     weights = stacked(kernel, 0)
     cells = jnp.concatenate([x[i : i + 2, j : j + 8].reshape(256, 128) for i, j in TAPS], axis=1)
     sums = lax.dot_general(cells, weights, (((1,), (1,)), ((), ())), preferred_element_type=F32)
@@ -156,11 +152,12 @@
 
 
 def level_c(own, pair, across, kernel, bias, skip_a, patch, skip_b, bottom, out_a, out_b, x, sem):
-    gy = lax.axis_index("gy")
+    gy, odd = lax.axis_index("gy"), lax.axis_index("gz") % 2
     write_b = pltpu.make_async_copy(skip_b, out_b, sem.at[0])
     write_b.start()
     inner = (gy == 1) | (gy == 2)
-    write_a = pltpu.make_async_copy(patch, out_a.at[:, jnp.where(gy == 1, 3, 0)], sem.at[1])
+    upper = jnp.where(gy == 2, 1, 0)
+    write_a = pltpu.make_async_copy(patch.at[upper], out_a.at[:, 3 * (1 - upper)], sem.at[1])
 
     @pl.when(inner)
     def _():
@@ -168,7 +165,6 @@
 
     x[:, 0] = jnp.zeros((3, 8, 256), BF16)
     x[:, 5] = jnp.zeros((3, 8, 256), BF16)
-    odd = lax.axis_index("gz") % 2
     x[1, 1:5] = jnp.concatenate([own[g] for g in range(4)], axis=-1)
     x[2 * (1 - odd), 1:5] = jnp.concatenate([pair[g] for g in range(4)], axis=-1)
     x[2 * odd, 1:5] = jnp.concatenate([across[odd, g] for g in range(4)], axis=-1)
@@ -206,7 +202,7 @@
     patch, skip_b, pooled_b, skip_a = local(
         level_b,
         (lax.all_gather(ship, "gy"), kernel_a, bias_a[None], jnp.swapaxes(kernel_b, 3, 4), bias_b[None], skip_a),
-        [((4, 32, 128), BF16), ((2, 8, 16, 64), BF16), ((1, 4, 8, 64), BF16), ((4, 4, 32, 128), BF16)],
+        [((2, 4, 32, 128), BF16), ((2, 8, 16, 64), BF16), ((1, 4, 8, 64), BF16), ((4, 4, 32, 128), BF16)],
         [((4, 10, 16, 128), BF16), ((128, 128), F32), ((64, 64), F32)],
         1 << 29,
         kept=(9,),

time: 59.7 us -> 59.5 us (level)
  no operation moved by 1% of the time
where the time goes in v7:
time: 59.5 us; the launch traced here: 59.2 us
  blocking collectives  47.9 us (81%)
  starting transfers between devices  5.31 us (9%)
  Pallas kernels  5.3 us (9%)
  between operations  0.71 us (1%)
    all_gather x2, blocking collectives, swap(): lax.all_gather(outward, ('gz', 'gy'), axis_index_groups=odd_groups(peers,...  23.4 us
    all_gather x1, blocking collectives, levels(): lax.all_gather(ship, 'gy')  13.2 us
    all_gather x1, blocking collectives, levels(): channels = lax.all_gather(pooled_b, 'gy', tiled=True)  9.1 us
    ppermute x2, starting transfers between devices, swap(): pair = lax.ppermute(inward, 'gz', [(i, i ^ 1) for i in range(peers)])  5.31 us
    pallas_call x5, Pallas kernels, local(): pl.pallas_call(body, out_shape=[jax.ShapeDtypeStruct(*out) for out in out...  5.3 us
    all_gather x1, blocking collectives, levels(): rows = lax.all_gather(rows, 'gy', axis_index_groups=even_groups(4))  2.17 us
  transfers between devices with their start and end apart: 2, of which 0 were waited for; matrix products, arithmetic and copies ran while one was open for 0% of the time, Pallas kernels for 0%

profile of v7, /device:TPU:40, one launch (start us, length us, event | category | flops | bytes accessed | tf_op | source)
XLA Modules:
  0.0 59.2 jit_solution(485437115029402176)
XLA Ops:
  0.6 0.9 %shard_map.94 = (bf16[4,4,32,128]{3,2,1,0:T(8,128)(2,1)S(1)}, bf16[3,4,32,128]{3,2,1,0:T(8,128)(2,1)S(1)}, bf16[3,4,32,128]{3,2,1,0:T(8,128)(2,1)S(1)}) custom-call(bf16[4,4,32,128]{3,2,1,0:T(8,128)(2,1)} %volume.1), custom_call_target="tpu_custom_call" | custom-call | bytes 1048576 | tf_op jit(solution)/shard_map/pallas_call | solution.py:36
  1.6 3.4 %collective-permute-start = (bf16[3,4,32,128]{3,2,1,0:T(8,128)(2,1)S(1)}, bf16[3,4,32,128]{3,2,1,0:T(8,128)(2,1)S(1)}, u32[]{:S(2)}, u32[]{:S(2)}) collective-permute-start(bf16[3,4,32,128]{3,2,1,0:T(8,128)(2,1)S(1)} %get-tuple-element.18), channel_id=1, source_target_pairs={{0,4},{4,0},{8,12},{12,8},{16,20},{20,16},{24,28},{28,24},{32,36},... | collective-permute-start | bytes 294920 | tf_op jit(solution)/shard_map/ppermute | solution.py:22
  5.0 14.6 %all-gather = bf16[6,4,32,128]{3,2,1,0:T(8,128)(2,1)S(1)} all-gather(bf16[3,4,32,128]{3,2,1,0:T(8,128)(2,1)S(1)} %get-tuple-element.19), channel_id=2, replica_groups={{4,8},{5,9},{6,10},{7,11},{12,16},{13,17},{14,18},{15,19},{20,24},{21,2..., dimensions={0}, use_global_device_ids=true | all-gather | bytes 294912 | tf_op jit(solution)/shard_map/all_gather | solution.py:23
  19.6 0.0 collective-permute-done.pair
  19.6 0.0 copy-start.2
  19.6 0.0 copy-start.4
  19.6 2.2 %all-gather.1 = bf16[4,10,32,128]{3,2,1,0:T(8,128)(2,1)S(1)} all-gather(bf16[2,10,32,128]{3,2,1,0:T(8,128)(2,1)S(1)} %get-tuple-element.21), channel_id=3, replica_groups={{0,1},{2,3},{4,5},{6,7},{8,9},{10,11},{12,13},{14,15},{16,17},{18,19},{..., dimensions={0}, use_global_device_ids=true | all-gather | bytes 491520 | tf_op jit(solution)/shard_map/all_gather | solution.py:194
  21.8 0.0 copy-done.2
  21.8 0.0 copy-done.4
  21.8 0.0 copy-start.3
  21.8 0.0 copy-start.5
  21.8 1.5 %shard_map.96 = (bf16[4,4,32,128]{3,2,1,0:T(8,128)(2,1)S(1)}, bf16[14,32,128]{2,1,0:T(8,128)(2,1)S(1)}) custom-call(bf16[10,4,32,128]{3,2,1,0:T(8,128)(2,1)S(1)} %get-tuple-element.20.wide, bf16[2,2,10,32,128]{4,3,2,1,0:T(8,128)(2,1)S(1)} %bitcast.9, bf16[3,3,3,128,128]{4,3,2,1,0:T(8,128)(2,1)S(1)} %copy-done.2, f32[1,128]{1,0:T(1,128)S(1)} %bitcast.14), custom_call_target="tpu_custom_call" | custom-call | flops 1073741824 | bytes 1048576 | tf_op jit(solution)/shard_map/pallas_call | solution.py:36
  23.4 0.0 copy-start
  23.4 0.0 copy-start.1
  23.4 13.2 %all-gather.2 = bf16[56,32,128]{2,1,0:T(8,128)(2,1)S(1)} all-gather(bf16[14,32,128]{2,1,0:T(8,128)(2,1)S(1)} %get-tuple-element.22), channel_id=4, replica_groups=mesh['gz'=128,'gy'=4] {'gy'}, dimensions={0}, use_global_device_ids=true | all-gather | bytes 573440 | tf_op jit(solution)/shard_map/all_gather | solution.py:204
  36.6 0.0 copy-done.3
  36.6 0.0 copy-done.5
  36.6 1.5 %shard_map.97 = (bf16[2,4,32,128]{3,2,1,0:T(8,128)(2,1)S(1)}, bf16[2,8,16,64]{3,2,1,0:T(8,128)(2,1)S(1)}, bf16[1,4,8,64]{3,2,1,0:T(8,128)(2,1)S(1)}, bf16[4,4,32,128]{3,2,1,0:T(8,128)(2,1)}) custom-call(bf16[4,14,32,128]{3,2,1,0:T(8,128)(2,1)S(1)} %bitcast.8, bf16[3,3,3,128,128]{4,3,2,1,0:T(8,128)(2,1)S(1)} %copy-done.2, f32[1,128]{1,0:T(1,128)S(1)} %bitcast.15, ...), custom_call_target="tpu_custom_call" | custom-call | flops 536870912 | bytes 1048576 | tf_op jit(solution)/shard_map/pallas_call | solution.py:36
  38.1 9.1 %all_gather.33.own = bf16[4,4,8,64]{3,2,1,0:T(8,128)(2,1)S(1)} all-gather(bf16[1,4,8,64]{3,2,1,0:T(8,128)(2,1)S(1)} %get-tuple-element.24), channel_id=1, replica_groups=mesh['gz'=128,'gy'=4] {'gy'}, dimensions={0}, use_global_device_ids=true | all-gather | bytes 20480 | tf_op jit(solution)/shard_map/all_gather | solution.py:211
  47.2 1.9 %collective-permute-start.1 = (bf16[4,4,8,64]{3,2,1,0:T(8,128)(2,1)S(1)}, bf16[4,4,8,64]{3,2,1,0:T(8,128)(2,1)S(1)}, u32[]{:S(2)}, u32[]{:S(2)}) collective-permute-start(bf16[4,4,8,64]{3,2,1,0:T(8,128)(2,1)S(1)} %all_gather.33.own), channel_id=1, source_target_pairs={{0,4},{4,0},{8,12},{12,8},{16,20},{20,16},{24,28},{28,24},{32,36},... | collective-permute-start | bytes 49160 | tf_op jit(solution)/shard_map/ppermute | solution.py:22
  49.1 8.8 %all-gather.3 = bf16[8,4,8,64]{3,2,1,0:T(8,128)(2,1)S(1)} all-gather(bf16[4,4,8,64]{3,2,1,0:T(8,128)(2,1)S(1)} %all_gather.33.own), channel_id=5, replica_groups={{4,8},{5,9},{6,10},{7,11},{12,16},{13,17},{14,18},{15,19},{20,24},{21,2..., dimensions={0}, use_global_device_ids=true | all-gather | bytes 49152 | tf_op jit(solution)/shard_map/all_gather | solution.py:23
  58.0 0.0 collective-permute-done.1.pair
  58.0 0.0 copy-done
  58.0 0.0 copy-done.1
  58.0 1.3 %shard_map.98 = (bf16[1,4,8,128]{3,2,1,0:T(8,128)(2,1)}, bf16[4,4,32,128]{3,2,1,0:T(8,128)(2,1)}, bf16[2,8,16,64]{3,2,1,0:T(8,128)(2,1)}) custom-call(bf16[4,4,8,64]{3,2,1,0:T(8,128)(2,1)S(1)} %all_gather.33.own, bf16[4,4,8,64]{3,2,1,0:T(8,128)(2,1)S(1)} %collective-permute-done.1.pair, ...), custom_call_target="tpu_custom_call", output_to_operand_aliasing={{1}: (5, {})} | custom-call | flops 134217728 | bytes 1048576 | tf_op jit(solution)/shard_map/pallas_call | solution.py:36
  (1 shorter events, 0.0 us)
Async XLA Ops:
  1.6 18.0 %collective-permute-start = (bf16[3,4,32,128]{3,2,1,0:T(8,128)(2,1)S(1)}, bf16[3,4,32,128]{3,2,1,0:T(8,128)(2,1)S(1)}, u32[]{:S(2)}, u32[]{:S(2)}) collective-permute-start(bf16[3,4,32,128]{3,2,1,0:T(8,128)(2,1)S(1)} %get-tuple-element.18), channel_id=1, source_target_pairs={{0,4},{4,0},{8,12},{12,8},{16,20},{20,16},{24,28},{28,24},{32,36},... | collective-permute-start | bytes 294920 | tf_op jit(solution)/shard_map/ppermute | solution.py:22
  19.6 2.2 %copy-start.2 = (bf16[3,3,3,128,128]{4,3,2,1,0:T(8,128)(2,1)S(1)}, bf16[3,3,3,128,128]{4,3,2,1,0:T(8,128)(2,1)}, u32[]{:S(2)}) copy-start(bf16[3,3,3,128,128]{4,3,2,1,0:T(8,128)(2,1)} %kernel_a.1) | copy-start | bytes 2654212
  19.6 2.2 %copy-start.4 = (f32[128]{0:T(128)S(1)}, f32[128]{0:T(128)}, u32[]{:S(2)}) copy-start(f32[128]{0:T(128)} %param.9) | copy-start | bytes 1540
  21.8 14.8 %copy-start.3 = (bf16[3,3,3,128,64]{3,4,2,1,0:T(8,128)(2,1)S(1)}, bf16[3,3,3,128,64]{3,4,2,1,0:T(8,128)(2,1)}, u32[]{:S(2)}) copy-start(bf16[3,3,3,128,64]{3,4,2,1,0:T(8,128)(2,1)} %param.10) | copy-start | bytes 1327108
  21.8 14.8 %copy-start.5 = (f32[64]{0:T(128)S(1)}, f32[64]{0:T(128)}, u32[]{:S(2)}) copy-start(f32[64]{0:T(128)} %param.11) | copy-start | bytes 772
  23.4 34.6 %copy-start = (bf16[3,3,3,256,128]{4,3,2,1,0:T(8,128)(2,1)S(1)}, bf16[3,3,3,256,128]{4,3,2,1,0:T(8,128)(2,1)}, u32[]{:S(2)}) copy-start(bf16[3,3,3,256,128]{4,3,2,1,0:T(8,128)(2,1)} %kernel.3) | copy-start | bytes 5308420
  23.4 34.6 %copy-start.1 = (f32[128]{0:T(128)S(1)}, f32[128]{0:T(128)}, u32[]{:S(2)}) copy-start(f32[128]{0:T(128)} %param.13) | copy-start | bytes 1540
  47.2 10.7 %collective-permute-start.1 = (bf16[4,4,8,64]{3,2,1,0:T(8,128)(2,1)S(1)}, bf16[4,4,8,64]{3,2,1,0:T(8,128)(2,1)S(1)}, u32[]{:S(2)}, u32[]{:S(2)}) collective-permute-start(bf16[4,4,8,64]{3,2,1,0:T(8,128)(2,1)S(1)} %all_gather.33.own), channel_id=1, source_target_pairs={{0,4},{4,0},{8,12},{12,8},{16,20},{20,16},{24,28},{28,24},{32,36},... | collective-permute-start | bytes 49160 | tf_op jit(solution)/shard_map/ppermute | solution.py:22
